TPU v7x, 128 devices: a whole 4x4x4 slice. The times are simulated.
128 devices in a mesh: inst: 8 (over y_hi, x), head: 16 (over y_lo, z, core).
Axes of the slice: x: 4, y: 4 (y_hi: 2, y_lo: 2; y = y_hi * 2 + y_lo), z: 4, core: 2. Of those that a mesh axis runs over, the one named last changes fastest.
Arguments:
- old_keys: bfloat16 [1024, 16, 64, 128], P('inst', 'head'), may hold values from -6 to 6
- old_values: bfloat16 [1024, 16, 64, 128], P('inst', 'head'), may hold values from -6 to 6
- old_block: int32 [1024], P('inst'), may hold values from -1 to 255, as said below
- new_slot: int32 [256], replicated, may hold values from 0 to 255, as said below
- lengths: int32 [64], replicated, may hold values from 1 to 16384, as said below
- queries: bfloat16 [64, 16, 8192], P(None, None, 'head'), may hold values from -240 to 240
- draft_keys: bfloat16 [64, 16, 1024], P('inst'), may hold values from -6 to 6
- draft_values: bfloat16 [64, 16, 1024], P('inst'), may hold values from -6 to 6
Outputs:
- moved_keys: bfloat16 [256, 16, 64, 128], P('inst', 'head')
- moved_values: bfloat16 [256, 16, 64, 128], P('inst', 'head')
- attended: bfloat16 [64, 16, 8192], P(None, None, 'head')
Inputs may be any that keep to these rules, and one draw needn't show every extreme that they name: ceil(lengths / 128) summed over the requests is exactly 256; the longest request has exactly 16384 tokens. `old_block`: every block 0 to 255 stands in exactly one old slot; the blocks fill all slots of 2 instances and all other slots hold -1. A permutation; block g goes to instance new_slot[g] // 32. At most 32 blocks go from one old instance to one new one, and in every draw some new instance receives all its 32 blocks from a single old instance.
All inputs are finite; a program needn't handle non-finite values.
Results may differ from a plain program's by a relative error of at most 0.004.
Values may be sent and summed in bfloat16 or wider, within the bound.
No kernel may reach another device: no remote copies, remote signals or barrier semaphores. Data moves between devices by JAX's collectives and lax.ppermute only.
A program may use at most 64 MiB of HBM per device.

v0:
```python
import math

import jax
import jax.numpy as jnp
from jax import lax
from jax.experimental import pallas as pl
from jax.experimental.pallas import tpu as pltpu
from jax.sharding import PartitionSpec as P


BLK = 128
masked = -1e30


COLS = 4


GROUPS_K = ((4, 3), (5, 6), (2,), (7,), (0,), (1,))
GROUPS_V = ((5, 3, 7), (1,), (4,), (2,), (6,), (0,))


def pack_body(old_block, new_slot, base, keys, values, *rest):
    count = len(GROUPS_K) + len(GROUPS_V)
    outs = rest[:count]
    vk, vv, zeros, origin, sems, load_sem = rest[count:]
    slots = keys.shape[0]
    total = new_slot.shape[0]
    per = zeros.shape[0]
    is_source = old_block[0] >= 0
    jobs = [(vk, out, group) for out, group in zip(outs, GROUPS_K)]
    jobs += [(vv, out, group) for out, group in zip(outs[len(GROUPS_K) :], GROUPS_V)]

    @pl.when(is_source)
    def _():
        load_k = pltpu.make_async_copy(keys, vk, load_sem.at[0])
        load_v = pltpu.make_async_copy(values, vv, load_sem.at[1])
        load_k.start()
        load_v.start()
        zeros[0] = jnp.zeros(zeros.shape[1:], zeros.dtype)

        def clear(t, c):
            origin[t] = -1
            return c

        lax.fori_loop(0, total, clear, 0, unroll=8)

        def note(i, c):
            origin[new_slot[jnp.maximum(old_block[i], 0)]] = i
            return c

        lax.fori_loop(0, slots, note, 0, unroll=8)
        load_k.wait()
        load_v.wait()
        for at, (cache, out, group) in enumerate(jobs):
            for g, p in enumerate(group):
                start = base[p]

                def send(j, c, cache=cache, out=out, at=at, g=g, start=start):
                    i = origin[start + j]

                    @pl.when(i >= 0)
                    def _():
                        pltpu.make_async_copy(cache.at[i], out.at[g * per + j], sems.at[at]).start()

                    @pl.when(i < 0)
                    def _():
                        pltpu.make_async_copy(zeros.at[0], out.at[g * per + j], sems.at[at]).start()

                    return c

                lax.fori_loop(0, per, send, 0, unroll=4)

    @pl.when(jnp.logical_not(is_source))
    def _():
        zeros[...] = jnp.zeros(zeros.shape, zeros.dtype)
        for at, (cache, out, group) in enumerate(jobs):
            for g in range(len(group)):
                pltpu.make_async_copy(zeros, out.at[pl.ds(g * per, per)], sems.at[at]).start()

    for at, (cache, out, group) in enumerate(jobs):
        pltpu.make_async_copy(out, out, sems.at[at]).wait()


def pack(old_block, new_slot, keys, values, inst, insts):
    total = new_slot.shape[0]
    per = total // insts
    step = jnp.arange(insts, dtype=jnp.int32)
    away = (inst // COLS) ^ (step % 2)
    column = (inst % COLS + step // 2) % COLS
    base = (away * COLS + column) * per
    groups = GROUPS_K + GROUPS_V
    anyspace = pl.BlockSpec(memory_space=pl.ANY)
    smem = pl.BlockSpec(memory_space=pltpu.SMEM)
    got = pl.pallas_call(
        pack_body,
        in_specs=[smem, smem, smem, anyspace, anyspace],
        out_specs=[anyspace] * len(groups),
        out_shape=[
            jax.ShapeDtypeStruct((per * len(g),) + keys.shape[1:], keys.dtype) for g in groups
        ],
        scratch_shapes=[
            pltpu.VMEM(keys.shape, keys.dtype),
            pltpu.VMEM(keys.shape, keys.dtype),
            pltpu.VMEM((per,) + keys.shape[1:], keys.dtype),
            pltpu.SMEM((total,), jnp.int32),
            pltpu.SemaphoreType.DMA((len(groups),)),
            pltpu.SemaphoreType.DMA((2,)),
        ],
        name="pack",
    )(old_block, new_slot, base, keys, values)
    return got[: len(GROUPS_K)], got[len(GROUPS_K) :]


def right(x):
    rows = lax.axis_size("inst") // COLS
    route = [(r * COLS + c, r * COLS + (c + 1) % COLS) for r in range(rows) for c in range(COLS)]
    return lax.ppermute(x, "inst", route)


def left(x):
    rows = lax.axis_size("inst") // COLS
    route = [(r * COLS + (c + 1) % COLS, r * COLS + c) for r in range(rows) for c in range(COLS)]
    return lax.ppermute(x, "inst", route)


def across(x):
    return lax.ppermute(x, "inst", [(i, i ^ COLS) for i in range(lax.axis_size("inst"))])


def vmem_call(body, outs, *args):
    vmem = pl.BlockSpec(memory_space=pltpu.VMEM)
    return pl.pallas_call(
        body,
        in_specs=[vmem] * len(args),
        out_specs=[vmem] * len(outs),
        out_shape=[jax.ShapeDtypeStruct(shape, args[0].dtype) for shape in outs],
    )(*args)


def merge_keys_body(from_left, from_right, k1n, k3f, k0n, k0f, o_right, o_left, near, cross):
    per = k1n.shape[0]
    o_right[...] = k1n[...] + from_left[:per]
    o_left[...] = k3f[...] + from_right[:per]
    near[...] = k0n[...] + from_right[per:]
    cross[...] = k0f[...] + from_left[per:]


def move_keys(from_left, from_right, groups):
    piece = groups[0].shape
    o_right, o_left, near, cross = vmem_call(
        merge_keys_body, [piece] * 4, from_left, from_right, *groups
    )
    a2 = right(o_right)
    b2 = left(o_left)
    crossed = across(cross + b2)
    return near + a2 + crossed


def merge_values_body(far, v2n, v1n, v3n, o_right, o_left, low, high):
    per = v1n.shape[0]
    cut = per // 2
    o_right[:cut] = v2n[:cut] + far[:cut]
    o_left[:cut] = v2n[cut:] + far[cut:per]
    low[...] = v1n[:cut] + far[per : per + cut]
    o_right[cut:] = v1n[cut:] + far[per + cut : 2 * per]
    o_left[cut:] = v3n[:cut] + far[2 * per : 2 * per + cut]
    high[...] = v3n[cut:] + far[2 * per + cut :]


def second_body(low, high, from_left, from_right, o_right, o_left):
    cut = low.shape[0]
    o_right[...] = low[...] + from_left[:cut]
    o_left[...] = high[...] + from_right[:cut]


def move_values(got, y0, groups):
    v2n, v1n, v3n, v0n = groups
    cut = v1n.shape[0] // 2
    piece = v1n.shape
    part = (cut,) + piece[1:]
    o_right, o_left, low, high = vmem_call(
        merge_values_body, [piece, piece, part, part], got, v2n, v1n, v3n
    )
    from_left = right(o_right)
    from_right = left(o_left)
    o_right, o_left = vmem_call(second_body, [part, part], low, high, from_left, from_right)
    e_lo = right(o_right)
    g_hi = left(o_left)
    return v0n + y0 + jnp.concatenate([e_lo + from_right[cut:], from_left[cut:] + g_hi])


def dot_t(x, y):
    return lax.dot_general(x, y, (((1,), (1,)), ((), ())), preferred_element_type=jnp.float32)


def attend_body(
    old_block, lengths, meta, q, k, v, ok, ov, dk, dv, packet,
    vq, vk, vv, vok, vov, scores, drafted, peak, total, acc, owner, live, sems,
):
    requests, draft, width = vq.shape
    head_dim = vk.shape[2]
    half = vk.shape[1]
    slots = vk.shape[0]
    heads = width // head_dim
    qrows = draft * heads
    insts = packet.shape[0]
    rows = requests // insts
    inv_root = 1.0 / math.sqrt(head_dim)
    is_source = old_block[0] >= 0
    first = meta[0]
    shift = meta[1]
    load_q = pltpu.make_async_copy(q, vq, sems.at[0])
    load_q.start()
    loads = [
        pltpu.make_async_copy(x, y, sems.at[1 + n])
        for n, (x, y) in enumerate(((k, vk), (ok, vok), (v, vv), (ov, vov)))
    ]

    @pl.when(is_source)
    def _():
        for load in loads:
            load.start()

        def per_request(r, g):
            size = lengths[r]

            def per_block(j, c):
                owner[g + j] = r
                live[g + j] = jnp.minimum(size - j * BLK, BLK)
                return c

            n = (size + BLK - 1) // BLK
            lax.fori_loop(0, n, per_block, 0)
            return g + n

        lax.fori_loop(0, requests, per_request, 0)

    def q_of(r):
        return jnp.concatenate(
            [vq[r, :, h * head_dim : (h + 1) * head_dim] for h in range(heads)], axis=0
        )

    lane = lax.broadcasted_iota(jnp.int32, (qrows, head_dim), 1)
    row = lax.broadcasted_iota(jnp.int32, (qrows, head_dim), 0)
    place = (lane + shift) % (2 * half)
    causal = lane <= row % draft
    blank = jnp.full((qrows, head_dim), masked, jnp.float32)

    def reset(r, c):
        peak[r] = blank
        return c

    lax.fori_loop(0, requests, reset, 0, unroll=4)
    load_q.wait()
    pad = jnp.zeros((2 * half - draft, head_dim), dk.dtype)
    for a in range(rows):
        s = dot_t(q_of(first + a), jnp.concatenate([dk[a], pad], axis=0)) * inv_root
        s = jnp.where(causal, s, masked)
        drafted[a] = s
        peak[first + a] = s

    @pl.when(is_source)
    def _():
        loads[0].wait()
        loads[1].wait()

        def score(n, c):
            for u in range(UNROLL):
                i = n * UNROLL + u
                g = jnp.maximum(old_block[i], 0)
                r = owner[g]
                key = jnp.concatenate([vk[i], vok[i]], axis=0)
                s = dot_t(q_of(r), key) * inv_root
                s = jnp.where(place < live[g], s, masked)
                scores[i] = s
                peak[r] = jnp.maximum(peak[r], s)
            return c

        lax.fori_loop(0, slots // UNROLL, score, 0)

    def settle(r, c):
        peak[r] = jnp.broadcast_to(jnp.max(peak[r], axis=1, keepdims=True), (qrows, head_dim))
        total[r] = jnp.zeros((qrows, head_dim), jnp.float32)
        acc[r] = jnp.zeros((qrows, head_dim), jnp.float32)
        return c

    lax.fori_loop(0, requests, settle, 0, unroll=2)
    for a in range(rows):
        w = jnp.exp(drafted[a] - peak[first + a])
        total[first + a] = w
        acc[first + a] = jnp.dot(
            w.astype(dv.dtype),
            jnp.concatenate([dv[a], pad], axis=0),
            preferred_element_type=jnp.float32,
        )

    @pl.when(is_source)
    def _():
        loads[2].wait()
        loads[3].wait()

        def gather(n, c):
            for u in range(UNROLL):
                i = n * UNROLL + u
                r = owner[jnp.maximum(old_block[i], 0)]
                w = jnp.exp(scores[i] - peak[r])
                value = jnp.concatenate([vv[i], vov[i]], axis=0)
                out = jnp.dot(w.astype(vv.dtype), value, preferred_element_type=jnp.float32)
                total[r] += w
                acc[r] += out
            return c

        lax.fori_loop(0, slots // UNROLL, gather, 0)

    def finish(d, c):
        stat = jnp.zeros((qrows, head_dim), jnp.float32)
        for a in range(rows):
            r = d * rows + a
            l = jnp.sum(total[r], axis=1, keepdims=True)
            seen = l > 0
            safe = jnp.where(seen, l, 1.0)
            packet[d, a * qrows : (a + 1) * qrows, :] = (acc[r] / safe).astype(packet.dtype)
            level = jnp.where(seen, peak[r] + jnp.log(safe), masked)
            hi = level.astype(jnp.bfloat16).astype(jnp.float32)
            mid = (level - hi).astype(jnp.bfloat16).astype(jnp.float32)
            low = level - hi - mid
            stat = jnp.where(lane == 3 * a, hi, stat)
            stat = jnp.where(lane == 3 * a + 1, mid, stat)
            stat = jnp.where(lane == 3 * a + 2, low, stat)
        packet[d, rows * qrows :, :] = stat.astype(packet.dtype)
        return c

    lax.fori_loop(0, insts, finish, 0)


UNROLL = 4


def attend(old_block, lengths, meta, queries, keys, values, other_k, other_v, dk, dv, insts):
    requests, draft, width = queries.shape
    head_dim = keys.shape[2]
    qrows = draft * width // head_dim
    rows = requests // insts
    anyspace = pl.BlockSpec(memory_space=pl.ANY)
    smem = pl.BlockSpec(memory_space=pltpu.SMEM)
    vmem = pl.BlockSpec(memory_space=pltpu.VMEM)
    bf16 = jnp.bfloat16
    state = pltpu.VMEM((requests, qrows, head_dim), jnp.float32)
    return pl.pallas_call(
        attend_body,
        in_specs=[smem] * 3 + [anyspace] * 5 + [vmem] * 2,
        out_specs=vmem,
        out_shape=jax.ShapeDtypeStruct((insts, (rows + 1) * qrows, head_dim), bf16),
        scratch_shapes=[pltpu.VMEM(queries.shape, bf16)]
        + [pltpu.VMEM(keys.shape, bf16)] * 4
        + [
            pltpu.VMEM((keys.shape[0], qrows, head_dim), jnp.float32),
            pltpu.VMEM((rows, qrows, head_dim), jnp.float32),
            state,
            state,
            state,
            pltpu.SMEM((TOTAL,), jnp.int32),
            pltpu.SMEM((TOTAL,), jnp.int32),
            pltpu.SemaphoreType.DMA((5,)),
        ],
        name="attend",
    )(old_block, lengths, meta, queries, keys, values, other_k, other_v, dk, dv)


TOTAL = 256


def join_body(got, out):
    insts, _, head_dim = got.shape
    rows = out.shape[1]
    draft = out.shape[2]
    heads = out.shape[3] // head_dim
    qrows = draft * heads
    lane = lax.broadcasted_iota(jnp.int32, (qrows, head_dim), 1)
    stats = [got[s, rows * qrows :, :].astype(jnp.float32) for s in range(insts)]
    for a in range(rows):
        mine = (lane >= 3 * a) & (lane < 3 * a + 3)
        level = [
            jnp.sum(jnp.where(mine, stat, 0.0), axis=1, keepdims=True) for stat in stats
        ]
        top = level[0]
        for x in level[1:]:
            top = jnp.maximum(top, x)
        total = jnp.zeros((qrows, 1), jnp.float32)
        acc = jnp.zeros((qrows, head_dim), jnp.float32)
        for s in range(insts):
            share = jnp.exp(level[s] - top)
            total = total + share
            acc = acc + share * got[s, a * qrows : (a + 1) * qrows, :].astype(jnp.float32)
        res = (acc / total).astype(out.dtype)
        for d in range(insts):
            for h in range(heads):
                out[d, a, :, h * head_dim : (h + 1) * head_dim] = res[h * draft : (h + 1) * draft]


def join(got, rows, draft, width):
    insts = got.shape[0]
    vmem = pl.BlockSpec(memory_space=pltpu.VMEM)
    return pl.pallas_call(
        join_body,
        in_specs=[vmem],
        out_specs=vmem,
        out_shape=jax.ShapeDtypeStruct((insts, rows, draft, width), got.dtype),
        name="join",
    )(got)


def spread(x):
    return lax.all_to_all(x, "inst", split_axis=0, concat_axis=0, tiled=True)


def move_and_attend(
    old_keys, old_values, old_block, new_slot, lengths, queries, draft_keys, draft_values
):
    insts = lax.axis_size("inst")
    inst = lax.axis_index("inst")
    me_head = lax.axis_index("head")
    _, entries, half, head_dim = old_keys.shape
    keys = old_keys.reshape(-1, half, head_dim)
    values = old_values.reshape(-1, half, head_dim)
    blocks = new_slot.shape[0]
    requests = queries.shape[0]
    rows = requests // insts
    swap = [(i, i ^ 1) for i in range(lax.axis_size("head"))]
    other_k = lax.ppermute(keys, "head", swap)
    other_v = lax.ppermute(values, "head", swap)

    out_k, out_v = pack(old_block, new_slot, keys, values, inst, insts)
    queries, out_k, out_v = lax.optimization_barrier((queries, out_k, out_v))
    shape = (blocks // insts, entries, half, head_dim)
    far = across(out_v[0])
    from_left = right(out_k[0])
    from_right = left(out_k[1])
    near = across(out_v[1])

    kv_head = me_head // 2
    dk = lax.dynamic_slice_in_dim(draft_keys, kv_head * head_dim, head_dim, 2)
    dv = lax.dynamic_slice_in_dim(draft_values, kv_head * head_dim, head_dim, 2)
    meta = jnp.stack([inst * rows, me_head % 2 * half])
    packet = attend(
        old_block, lengths, meta, queries, keys, values, other_k, other_v, dk, dv, insts
    )
    packet, rest_k, rest_v = lax.optimization_barrier((packet, out_k[2:], out_v[2:]))
    moved_keys = move_keys(from_left, from_right, rest_k).reshape(shape)
    moved_values = move_values(far, near, rest_v).reshape(shape)
    got = spread(packet)
    mine = join(got, rows, queries.shape[1], queries.shape[2])
    attended = spread(mine).reshape(queries.shape)
    return moved_keys, moved_values, attended


def solution(mesh):
    placed = (
        P("inst", "head", None, None),
        P("inst", "head", None, None),
        P("inst"),
        P(),
        P(),
        P(None, None, "head"),
        P("inst", None, None),
        P("inst", None, None),
    )
    return jax.shard_map(
        move_and_attend,
        mesh=mesh,
        in_specs=placed,
        out_specs=(
            P("inst", "head", None, None),
            P("inst", "head", None, None),
            P(None, None, "head"),
        ),
        check_vma=False,
    )
```

profile of v0, /device:TPU:0, one launch (start us, length us, event | category | flops | bytes accessed | tf_op | source)
XLA Modules:
  0.0 113.9 jit_solution(17282461067873875284)
XLA Ops:
  0.6 0.1 collective-permute-start.2
  0.7 0.5 collective-permute-start.3
  1.2 0.5 fusion.6.base
  1.8 4.1 %pack.1 = (bf16[64,64,128]{2,1,0:T(8,128)(2,1)}, bf16[64,64,128]{2,1,0:T(8,128)(2,1)}, bf16[32,64,128]{2,1,0:T(8,128)(2,1)}, bf16[32,64,128]{2,1,0:T(8,128)(2,1)...) custom-call(s32[128]{0:T(128)} %old_block.3, ...), custom_call_target="tpu_custom_call" | custom-call | tf_op jit(solution)/shard_map/pack/pallas_call | solution.py:94
  5.9 5.4 %collective-permute-start.8 = (bf16[96,64,128]{2,1,0:T(8,128)(2,1)}, bf16[96,64,128]{2,1,0:T(8,128)(2,1)}, u32[]{:S(2)}, u32[]{:S(2)}) collective-permute-start(bf16[96,64,128]{2,1,0:T(8,128)(2,1)} %get-tuple-element.80), channel_id=1, source_target_pairs={{0,64},{16,80},{32,96},{48,112},{64,0},{80,16},{96,32},{112,48},{1... | collective-permute-start | bytes 4718600 | tf_op jit(solution)/shard_map/ppermute | solution.py:127
  11.4 0.0 collective-permute-start
  11.4 3.2 %collective-permute-start.1 = (bf16[64,64,128]{2,1,0:T(8,128)(2,1)}, bf16[64,64,128]{2,1,0:T(8,128)(2,1)}, u32[]{:S(2)}, u32[]{:S(2)}) collective-permute-start(bf16[64,64,128]{2,1,0:T(8,128)(2,1)} %get-tuple-element.60), channel_id=1, source_target_pairs={{16,0},{32,16},{48,32},{0,48},{80,64},{96,80},{112,96},{64,112},{1... | collective-permute-start | bytes 3145736 | tf_op jit(solution)/shard_map/ppermute | solution.py:123
  14.6 0.6 pad_add_fusion.meta
  15.2 1.4 %constant_dynamic-slice_fusion = (bf16[8,16,128]{2,1,0:T(8,128)(2,1)}, bf16[8,16,128]{2,1,0:T(8,128)(2,1)}) fusion(bf16[8,16,1024]{2,1,0:T(8,128)(2,1)} %param.15, s32[]{:T(128)S(6)} %select_n.44, bf16[8,16,1024]{2,1,0:T(8,128)(2,1)} %param.14), kind=kLoop, calls=%fused_computation.19 | loop fusion | bytes 131076 | tf_op jit(solution)/shard_map/dynamic_slice | solution.py:443
  16.6 0.0 collective-permute-done.2.ok
  16.6 0.0 collective-permute-done.3.ov
  16.6 1.3 %copy-done.1 = bf16[128,64,128]{2,1,0:T(8,128)(2,1)} copy-done((bf16[128,64,128]{2,1,0:T(8,128)(2,1)}, bf16[128,64,128]{2,1,0:T(8,128)(2,1)S(1)}, u32[]{:S(2)}) %copy-start.1) | copy-done | bytes 2097176
  17.9 8.3 %attend.1 = bf16[8,576,128]{2,1,0:T(8,128)(2,1)} custom-call(s32[128]{0:T(128)} %old_block.3, s32[64]{0:T(128)} %lengths.1, s32[2]{0:T(128)} %pad_add_fusion.meta, bf16[64,16,512]{2,1,0:T(8,128)(2,1)} %q, bf16[128,64,128]{2,1,0:T(8,128)(2,1)} %bitcast.15, bf16[128,64,128]{2,1,0:T(8,128)(2,1)} %bitcast.18, bf16[128,64,128]{2,1,0:T(8,128)(2,1)} %copy-done.1, ...), custom_call_target="tpu_custom_call" | custom-call | tf_op jit(solution)/shard_map/attend/pallas_call | solution.py:349
  26.2 15.1 %all-to-all-start = ((bf16[8,576,128]{2,1,0:T(8,128)(2,1)}), bf16[8,576,128]{2,1,0:T(8,128)(2,1)S(1)}, u32[]{:S(2)}, u32[]{:S(2)}) async-start(bf16[8,576,128]{2,1,0:T(8,128)(2,1)} %attend.1), calls=%async_computation | async-start | bytes 2359296 | tf_op jit(solution)/shard_map/all_to_all | solution.py:414
  41.3 11.7 %collective-permute-done.8.far = bf16[96,64,128]{2,1,0:T(8,128)(2,1)} collective-permute-done((bf16[96,64,128]{2,1,0:T(8,128)(2,1)}, bf16[96,64,128]{2,1,0:T(8,128)(2,1)}, u32[]{:S(2)}, u32[]{:S(2)}) %collective-permute-start.8) | collective-permute-done | bytes 1572896 | tf_op jit(solution)/shard_map/ppermute | solution.py:127
  53.0 3.4 %shard_map.104 = (bf16[32,64,128]{2,1,0:T(8,128)(2,1)}, bf16[32,64,128]{2,1,0:T(8,128)(2,1)}, bf16[16,64,128]{2,1,0:T(8,128)(2,1)}, bf16[16,64,128]{2,1,0:T(8,128)(2,1)}) custom-call(bf16[96,64,128]{2,1,0:T(8,128)(2,1)} %collective-permute-done.8.far, bf16[32,64,128]{2,1,0:T(8,128)(2,1)} %get-tuple-element.81.v2n, ...), custom_call_target="tpu_custom_call" | custom-call | tf_op jit(solution)/shard_map/pallas_call | solution.py:132
  56.3 0.0 collective-permute-start.9
  56.4 3.5 %collective-permute-start.10 = (bf16[32,64,128]{2,1,0:T(8,128)(2,1)}, bf16[32,64,128]{2,1,0:T(8,128)(2,1)S(1)}, u32[]{:S(2)}, u32[]{:S(2)}) collective-permute-start(bf16[32,64,128]{2,1,0:T(8,128)(2,1)} %get-tuple-element.87), channel_id=1, source_target_pairs={{16,0},{32,16},{48,32},{0,48},{80,64},{96,80},{112,96},{64,112},{1... | collective-permute-start | bytes 1572872 | tf_op jit(solution)/shard_map/ppermute | solution.py:123
  59.9 0.0 collective-permute-done.from_left
  59.9 0.0 collective-permute-done.1.from_right
  59.9 1.0 copy-done.6
  60.9 3.9 %shard_map.103 = (bf16[32,64,128]{2,1,0:T(8,128)(2,1)}, bf16[32,64,128]{2,1,0:T(8,128)(2,1)}, bf16[32,64,128]{2,1,0:T(8,128)(2,1)}, bf16[32,64,128]{2,1,0:T(8,128)(2,1)}) custom-call(bf16[64,64,128]{2,1,0:T(8,128)(2,1)} %copy-done.6, bf16[64,64,128]{2,1,0:T(8,128)(2,1)} %collective-permute-done.1.from_right, bf16[32,64,128]{2,1,0:T(8,128)(2,1)} %get-tuple-element.70.k1n, ...), custom_call_target="tpu_custom_call" | custom-call | tf_op jit(solution)/shard_map/pallas_call | solution.py:132
  64.8 2.0 %collective-permute-start.5 = (bf16[32,64,128]{2,1,0:T(8,128)(2,1)}, bf16[32,64,128]{2,1,0:T(8,128)(2,1)S(1)}, u32[]{:S(2)}, u32[]{:S(2)}) collective-permute-start(bf16[32,64,128]{2,1,0:T(8,128)(2,1)} %get-tuple-element.77), channel_id=1, source_target_pairs={{16,0},{32,16},{48,32},{0,48},{80,64},{96,80},{112,96},{64,112},{1... | collective-permute-start | bytes 1572872 | tf_op jit(solution)/shard_map/ppermute | solution.py:123
  66.8 1.7 %collective-permute-done.9.from_left = bf16[32,64,128]{2,1,0:T(8,128)(2,1)S(1)} collective-permute-done((bf16[32,64,128]{2,1,0:T(8,128)(2,1)}, bf16[32,64,128]{2,1,0:T(8,128)(2,1)S(1)}, u32[]{:S(2)}, u32[]{:S(2)}) %collective-permute-start.9) | collective-permute-done | bytes 524320 | tf_op jit(solution)/shard_map/ppermute | solution.py:117
  68.5 4.7 %collective-permute-done.10.from_right = bf16[32,64,128]{2,1,0:T(8,128)(2,1)S(1)} collective-permute-done((bf16[32,64,128]{2,1,0:T(8,128)(2,1)}, bf16[32,64,128]{2,1,0:T(8,128)(2,1)S(1)}, u32[]{:S(2)}, u32[]{:S(2)}) %collective-permute-start.10) | collective-permute-done | bytes 524320 | tf_op jit(solution)/shard_map/ppermute | solution.py:123
  73.2 0.8 copy-done.4
  74.0 2.3 %shard_map.105 = (bf16[16,64,128]{2,1,0:T(8,128)(2,1)}, bf16[16,64,128]{2,1,0:T(8,128)(2,1)}) custom-call(bf16[16,64,128]{2,1,0:T(8,128)(2,1)} %get-tuple-element.84.low, bf16[16,64,128]{2,1,0:T(8,128)(2,1)} %get-tuple-element.85.high, bf16[32,64,128]{2,1,0:T(8,128)(2,1)} %copy-done.2, bf16[32,64,128]{2,1,0:T(8,128)(2,1)} %copy-done.4), custom_call_target="tpu_custom_call" | custom-call | tf_op jit(solution)/shard_map/pallas_call | solution.py:132
  76.3 2.0 %collective-permute-start.11 = (bf16[16,64,128]{2,1,0:T(8,128)(2,1)}, bf16[16,64,128]{2,1,0:T(8,128)(2,1)S(1)}, u32[]{:S(2)}, u32[]{:S(2)}) collective-permute-start(bf16[16,64,128]{2,1,0:T(8,128)(2,1)} %get-tuple-element.88), channel_id=1, source_target_pairs={{0,16},{16,32},{32,48},{48,0},{64,80},{80,96},{96,112},{112,64},{1... | collective-permute-start | bytes 786440 | tf_op jit(solution)/shard_map/ppermute | solution.py:117
  78.4 4.0 %collective-permute-start.7 = (bf16[32,64,128]{2,1,0:T(8,128)(2,1)}, bf16[32,64,128]{2,1,0:T(8,128)(2,1)}, u32[]{:S(2)}, u32[]{:S(2)}) collective-permute-start(bf16[32,64,128]{2,1,0:T(8,128)(2,1)} %get-tuple-element.79), channel_id=1, source_target_pairs={{0,64},{16,80},{32,96},{48,112},{64,0},{80,16},{96,32},{112,48},{1... | collective-permute-start | bytes 1572872 | tf_op jit(solution)/shard_map/ppermute | solution.py:127
  82.3 1.2 %collective-permute-start.12 = (bf16[16,64,128]{2,1,0:T(8,128)(2,1)}, bf16[16,64,128]{2,1,0:T(8,128)(2,1)}, u32[]{:S(2)}, u32[]{:S(2)}) collective-permute-start(bf16[16,64,128]{2,1,0:T(8,128)(2,1)} %get-tuple-element.89), channel_id=1, source_target_pairs={{16,0},{32,16},{48,32},{0,48},{80,64},{96,80},{112,96},{64,112},{1... | collective-permute-start | bytes 786440 | tf_op jit(solution)/shard_map/ppermute | solution.py:123
  83.5 0.8 collective-permute-start.4
  84.4 0.1 collective-permute-done.5
  84.5 1.2 %add.63 = bf16[32,64,128]{2,1,0:T(8,128)(2,1)S(1)} add(bf16[32,64,128]{2,1,0:T(8,128)(2,1)} %get-tuple-element.76, bf16[32,64,128]{2,1,0:T(8,128)(2,1)S(1)} %collective-permute-done.5) | non-fusion elementwise | flops 262144 | bytes 1572864 | tf_op jit(solution)/shard_map/add | solution.py:155
  85.7 0.0 copy-start.5
  85.7 0.0 copy-start.3
  85.7 4.1 %collective-permute-start.6 = (bf16[32,64,128]{2,1,0:T(8,128)(2,1)S(1)}, bf16[32,64,128]{2,1,0:T(8,128)(2,1)}, u32[]{:S(2)}, u32[]{:S(2)}) collective-permute-start(bf16[32,64,128]{2,1,0:T(8,128)(2,1)S(1)} %add.63), channel_id=1, source_target_pairs={{0,64},{16,80},{32,96},{48,112},{64,0},{80,16},{96,32},{112,48},{1... | collective-permute-start | bytes 1572872 | tf_op jit(solution)/shard_map/ppermute | solution.py:127
  89.8 1.0 copy-done
  90.8 3.1 %join.1 = bf16[8,8,16,512]{3,2,1,0:T(8,128)(2,1)} custom-call(bf16[8,576,128]{2,1,0:T(8,128)(2,1)} %copy-done), custom_call_target="tpu_custom_call" | custom-call | tf_op jit(solution)/shard_map/join/pallas_call | solution.py:404
  93.9 3.7 %all-to-all-start.1 = ((bf16[8,8,16,512]{3,2,1,0:T(8,128)(2,1)}), bf16[8,8,16,512]{3,2,1,0:T(8,128)(2,1)S(1)}, u32[]{:S(2)}, u32[]{:S(2)}) async-start(bf16[8,8,16,512]{3,2,1,0:T(8,128)(2,1)} %join.1), calls=%async_computation.1 | async-start | bytes 2097152 | tf_op jit(solution)/shard_map/all_to_all | solution.py:414
  97.6 0.0 collective-permute-done.11
  97.7 0.0 collective-permute-done.12
  97.7 1.0 slice_add_fusion
  98.7 0.0 collective-permute-done.7
  98.7 1.9 %fusion = bf16[32,1,64,128]{3,2,1,0:T(8,128)(2,1)} fusion(bf16[16,64,128]{2,1,0:T(8,128)(2,1)S(1)} %slice_add_fusion, bf16[16,64,128]{2,1,0:T(8,128)(2,1)S(1)} %slice_add_fusion.1, bf16[32,64,128]{2,1,0:T(8,128)(2,1)S(1)} %copy-done.7, bf16[32,64,128]{2,1,0:T(8,128)(2,1)} %collective-permute-done.7), kind=kLoop, calls=%fused_computation.1 | loop fusion | flops 786432 | bytes 2097152
  100.7 0.0 collective-permute-done.4
  100.7 10.2 %collective-permute-done.6 = bf16[32,64,128]{2,1,0:T(8,128)(2,1)} collective-permute-done((bf16[32,64,128]{2,1,0:T(8,128)(2,1)S(1)}, bf16[32,64,128]{2,1,0:T(8,128)(2,1)}, u32[]{:S(2)}, u32[]{:S(2)}) %collective-permute-start.6) | collective-permute-done | bytes 524320 | tf_op jit(solution)/shard_map/ppermute | solution.py:127
  110.9 2.1 %add_bitcast_fusion = bf16[32,1,64,128]{3,2,1,0:T(8,128)(2,1)} fusion(bf16[32,64,128]{2,1,0:T(8,128)(2,1)} %collective-permute-done.6, bf16[32,64,128]{2,1,0:T(8,128)(2,1)S(1)} %copy-done.8, bf16[32,64,128]{2,1,0:T(8,128)(2,1)} %collective-permute-done.4), kind=kLoop, calls=%fused_computation.2 | loop fusion | flops 524288 | bytes 2097152
  113.0 1.0 copy.14
  (15 shorter events, 0.1 us)
Async XLA Ops:
  0.6 16.0 %collective-permute-start.2 = (bf16[128,64,128]{2,1,0:T(8,128)(2,1)}, bf16[128,64,128]{2,1,0:T(8,128)(2,1)S(1)}, u32[]{:S(2)}, u32[]{:S(2)}) collective-permute-start(bf16[128,64,128]{2,1,0:T(8,128)(2,1)} %bitcast.13), channel_id=1, source_target_pairs={{0,1},{1,0},{2,3},{3,2},{4,5},{5,4},{6,7},{7,6},{8,9},{9,8},{10,11... | collective-permute-start | bytes 6291464 | tf_op jit(solution)/shard_map/ppermute | solution.py:430
  0.7 15.9 %collective-permute-start.3 = (bf16[128,64,128]{2,1,0:T(8,128)(2,1)}, bf16[128,64,128]{2,1,0:T(8,128)(2,1)}, u32[]{:S(2)}, u32[]{:S(2)}) collective-permute-start(bf16[128,64,128]{2,1,0:T(8,128)(2,1)} %bitcast.16), channel_id=1, source_target_pairs={{0,1},{1,0},{2,3},{3,2},{4,5},{5,4},{6,7},{7,6},{8,9},{9,8},{10,11... | collective-permute-start | bytes 6291464 | tf_op jit(solution)/shard_map/ppermute | solution.py:431
  5.9 47.0 %collective-permute-start.8 = (bf16[96,64,128]{2,1,0:T(8,128)(2,1)}, bf16[96,64,128]{2,1,0:T(8,128)(2,1)}, u32[]{:S(2)}, u32[]{:S(2)}) collective-permute-start(bf16[96,64,128]{2,1,0:T(8,128)(2,1)} %get-tuple-element.80), channel_id=1, source_target_pairs={{0,64},{16,80},{32,96},{48,112},{64,0},{80,16},{96,32},{112,48},{1... | collective-permute-start | bytes 4718600 | tf_op jit(solution)/shard_map/ppermute | solution.py:127
  11.4 48.5 %collective-permute-start = (bf16[64,64,128]{2,1,0:T(8,128)(2,1)}, bf16[64,64,128]{2,1,0:T(8,128)(2,1)S(1)}, u32[]{:S(2)}, u32[]{:S(2)}) collective-permute-start(bf16[64,64,128]{2,1,0:T(8,128)(2,1)} %get-tuple-element.59), channel_id=1, source_target_pairs={{0,16},{16,32},{32,48},{48,0},{64,80},{80,96},{96,112},{112,64},{1... | collective-permute-start | bytes 3145736 | tf_op jit(solution)/shard_map/ppermute | solution.py:117
  11.4 48.5 %collective-permute-start.1 = (bf16[64,64,128]{2,1,0:T(8,128)(2,1)}, bf16[64,64,128]{2,1,0:T(8,128)(2,1)}, u32[]{:S(2)}, u32[]{:S(2)}) collective-permute-start(bf16[64,64,128]{2,1,0:T(8,128)(2,1)} %get-tuple-element.60), channel_id=1, source_target_pairs={{16,0},{32,16},{48,32},{0,48},{80,64},{96,80},{112,96},{64,112},{1... | collective-permute-start | bytes 3145736 | tf_op jit(solution)/shard_map/ppermute | solution.py:123
  16.6 1.3 %copy-start.1 = (bf16[128,64,128]{2,1,0:T(8,128)(2,1)}, bf16[128,64,128]{2,1,0:T(8,128)(2,1)S(1)}, u32[]{:S(2)}) copy-start(bf16[128,64,128]{2,1,0:T(8,128)(2,1)S(1)} %collective-permute-done.2.ok) | copy-start | bytes 6291460
  26.2 63.6 %all-to-all-start = ((bf16[8,576,128]{2,1,0:T(8,128)(2,1)}), bf16[8,576,128]{2,1,0:T(8,128)(2,1)S(1)}, u32[]{:S(2)}, u32[]{:S(2)}) async-start(bf16[8,576,128]{2,1,0:T(8,128)(2,1)} %attend.1), calls=%async_computation | async-start | bytes 2359296 | tf_op jit(solution)/shard_map/all_to_all | solution.py:414
  56.3 12.1 %collective-permute-start.9 = (bf16[32,64,128]{2,1,0:T(8,128)(2,1)}, bf16[32,64,128]{2,1,0:T(8,128)(2,1)S(1)}, u32[]{:S(2)}, u32[]{:S(2)}) collective-permute-start(bf16[32,64,128]{2,1,0:T(8,128)(2,1)} %get-tuple-element.86), channel_id=1, source_target_pairs={{0,16},{16,32},{32,48},{48,0},{64,80},{80,96},{96,112},{112,64},{1... | collective-permute-start | bytes 1572872 | tf_op jit(solution)/shard_map/ppermute | solution.py:117
  56.4 16.9 %collective-permute-start.10 = (bf16[32,64,128]{2,1,0:T(8,128)(2,1)}, bf16[32,64,128]{2,1,0:T(8,128)(2,1)S(1)}, u32[]{:S(2)}, u32[]{:S(2)}) collective-permute-start(bf16[32,64,128]{2,1,0:T(8,128)(2,1)} %get-tuple-element.87), channel_id=1, source_target_pairs={{16,0},{32,16},{48,32},{0,48},{80,64},{96,80},{112,96},{64,112},{1... | collective-permute-start | bytes 1572872 | tf_op jit(solution)/shard_map/ppermute | solution.py:123
  59.9 1.0 copy-start.6
  64.8 19.7 %collective-permute-start.5 = (bf16[32,64,128]{2,1,0:T(8,128)(2,1)}, bf16[32,64,128]{2,1,0:T(8,128)(2,1)S(1)}, u32[]{:S(2)}, u32[]{:S(2)}) collective-permute-start(bf16[32,64,128]{2,1,0:T(8,128)(2,1)} %get-tuple-element.77), channel_id=1, source_target_pairs={{16,0},{32,16},{48,32},{0,48},{80,64},{96,80},{112,96},{64,112},{1... | collective-permute-start | bytes 1572872 | tf_op jit(solution)/shard_map/ppermute | solution.py:123
  68.5 4.8 %copy-start.2 = (bf16[32,64,128]{2,1,0:T(8,128)(2,1)}, bf16[32,64,128]{2,1,0:T(8,128)(2,1)S(1)}, u32[]{:S(2)}) copy-start(bf16[32,64,128]{2,1,0:T(8,128)(2,1)S(1)} %collective-permute-done.9.from_left) | copy-start | bytes 1572868
  73.2 0.8 copy-start.4
  76.3 21.3 %collective-permute-start.11 = (bf16[16,64,128]{2,1,0:T(8,128)(2,1)}, bf16[16,64,128]{2,1,0:T(8,128)(2,1)S(1)}, u32[]{:S(2)}, u32[]{:S(2)}) collective-permute-start(bf16[16,64,128]{2,1,0:T(8,128)(2,1)} %get-tuple-element.88), channel_id=1, source_target_pairs={{0,16},{16,32},{32,48},{48,0},{64,80},{80,96},{96,112},{112,64},{1... | collective-permute-start | bytes 786440 | tf_op jit(solution)/shard_map/ppermute | solution.py:117
  78.4 20.4 %collective-permute-start.7 = (bf16[32,64,128]{2,1,0:T(8,128)(2,1)}, bf16[32,64,128]{2,1,0:T(8,128)(2,1)}, u32[]{:S(2)}, u32[]{:S(2)}) collective-permute-start(bf16[32,64,128]{2,1,0:T(8,128)(2,1)} %get-tuple-element.79), channel_id=1, source_target_pairs={{0,64},{16,80},{32,96},{48,112},{64,0},{80,16},{96,32},{112,48},{1... | collective-permute-start | bytes 1572872 | tf_op jit(solution)/shard_map/ppermute | solution.py:127
  82.3 15.3 %collective-permute-start.12 = (bf16[16,64,128]{2,1,0:T(8,128)(2,1)}, bf16[16,64,128]{2,1,0:T(8,128)(2,1)}, u32[]{:S(2)}, u32[]{:S(2)}) collective-permute-start(bf16[16,64,128]{2,1,0:T(8,128)(2,1)} %get-tuple-element.89), channel_id=1, source_target_pairs={{16,0},{32,16},{48,32},{0,48},{80,64},{96,80},{112,96},{64,112},{1... | collective-permute-start | bytes 786440 | tf_op jit(solution)/shard_map/ppermute | solution.py:123
  83.5 17.1 %collective-permute-start.4 = (bf16[32,64,128]{2,1,0:T(8,128)(2,1)}, bf16[32,64,128]{2,1,0:T(8,128)(2,1)}, u32[]{:S(2)}, u32[]{:S(2)}) collective-permute-start(bf16[32,64,128]{2,1,0:T(8,128)(2,1)} %get-tuple-element.75), channel_id=1, source_target_pairs={{0,16},{16,32},{32,48},{48,0},{64,80},{80,96},{96,112},{112,64},{1... | collective-permute-start | bytes 1572872 | tf_op jit(solution)/shard_map/ppermute | solution.py:117
  85.7 11.9 %copy-start.5 = (bf16[32,64,128]{2,1,0:T(8,128)(2,1)S(1)}, bf16[32,64,128]{2,1,0:T(8,128)(2,1)}, u32[]{:S(2)}) copy-start(bf16[32,64,128]{2,1,0:T(8,128)(2,1)} %copy-done.4) | copy-start | bytes 1572868
  85.7 12.0 %copy-start.3 = (bf16[32,64,128]{2,1,0:T(8,128)(2,1)S(1)}, bf16[32,64,128]{2,1,0:T(8,128)(2,1)}, u32[]{:S(2)}) copy-start(bf16[32,64,128]{2,1,0:T(8,128)(2,1)} %copy-done.2) | copy-start | bytes 1572868
  85.7 25.1 %collective-permute-start.6 = (bf16[32,64,128]{2,1,0:T(8,128)(2,1)S(1)}, bf16[32,64,128]{2,1,0:T(8,128)(2,1)}, u32[]{:S(2)}, u32[]{:S(2)}) collective-permute-start(bf16[32,64,128]{2,1,0:T(8,128)(2,1)S(1)} %add.63), channel_id=1, source_target_pairs={{0,64},{16,80},{32,96},{48,112},{64,0},{80,16},{96,32},{112,48},{1... | collective-permute-start | bytes 1572872 | tf_op jit(solution)/shard_map/ppermute | solution.py:127
  89.8 1.0 copy-start
  93.9 4.8 %copy-start.7 = (bf16[32,64,128]{2,1,0:T(8,128)(2,1)S(1)}, bf16[32,64,128]{2,1,0:T(8,128)(2,1)}, u32[]{:S(2)}) copy-start(bf16[32,64,128]{2,1,0:T(8,128)(2,1)} %get-tuple-element.78) | copy-start | bytes 1572868
  93.9 19.0 %all-to-all-start.1 = ((bf16[8,8,16,512]{3,2,1,0:T(8,128)(2,1)}), bf16[8,8,16,512]{3,2,1,0:T(8,128)(2,1)S(1)}, u32[]{:S(2)}, u32[]{:S(2)}) async-start(bf16[8,8,16,512]{3,2,1,0:T(8,128)(2,1)} %join.1), calls=%async_computation.1 | async-start | bytes 2097152 | tf_op jit(solution)/shard_map/all_to_all | solution.py:414
  97.6 13.3 %copy-start.8 = (bf16[32,64,128]{2,1,0:T(8,128)(2,1)S(1)}, bf16[32,64,128]{2,1,0:T(8,128)(2,1)}, u32[]{:S(2)}) copy-start(bf16[32,64,128]{2,1,0:T(8,128)(2,1)} %get-tuple-element.74) | copy-start | bytes 1572868
where the time goes:
time: 115 us; the launch traced here: 114 us
  starting transfers between devices  45.7 us (40%)
  waiting for transfers between devices  28.4 us (25%)
  Pallas kernels  25.1 us (22%)
  other arithmetic  7.4 us (6%)
  local copies, waits for them, and re-layouts  6.47 us (6%)
    ppermute x3, waiting for transfers between devices, across(): lax.ppermute(x, 'inst', [(i, i ^ COLS) for i in range(lax.axis_size('inst...  21.9 us
    all_to_all x2, starting transfers between devices, spread(): return lax.all_to_all(x, 'inst', split_axis=0, concat_axis=0, tiled=True)  18.8 us
    ppermute x3, starting transfers between devices, across(): lax.ppermute(x, 'inst', [(i, i ^ COLS) for i in range(lax.axis_size('inst...  13.5 us
    ppermute x4, starting transfers between devices, left(): return lax.ppermute(x, 'inst', route)  10 us
    pallas_call x3, Pallas kernels, vmem_call(): pl.pallas_call(body, in_specs=[vmem] * len(args), out_specs=[vmem] * len(...  9.59 us
    pallas_call x1, Pallas kernels, attend(): pl.pallas_call(attend_body, in_specs=[smem] * 3 + [anyspace] * 5 + [vmem]...  8.32 us
    unnamed x19, local copies, waits for them, and re-layouts  5.07 us
    ppermute x4, waiting for transfers between devices, left(): return lax.ppermute(x, 'inst', route)  4.86 us
  transfers between devices with their start and end apart: 15, of which 5 were waited for; matrix products, arithmetic and copies ran while one was open for 8% of the time, Pallas kernels for 22%

commit v1 on v0

--- a/solution.py
+++ b/solution.py
@@ -81,13 +81,25 @@
         pltpu.make_async_copy(out, out, sems.at[at]).wait()
 
 
-def pack(old_block, new_slot, keys, values, inst, insts):
-    total = new_slot.shape[0]
-    per = total // insts
-    step = jnp.arange(insts, dtype=jnp.int32)
+def table_of(per, rows, half, head_dim):
+    insts = lax.axis_size("inst")
+    inst = lax.axis_index("inst")
+    me_head = lax.axis_index("head")
+    step = jnp.arange(16, dtype=jnp.int32)
     away = (inst // COLS) ^ (step % 2)
     column = (inst % COLS + step // 2) % COLS
     base = (away * COLS + column) * per
+    rest = jnp.where(
+        step == insts,
+        inst * rows,
+        jnp.where(step == insts + 1, me_head % 2 * half, me_head // 2 * head_dim),
+    )
+    return jnp.where(step < insts, base, rest)
+
+
+def pack(old_block, new_slot, base, keys, values, insts):
+    total = new_slot.shape[0]
+    per = total // insts
     groups = GROUPS_K + GROUPS_V
     anyspace = pl.BlockSpec(memory_space=pl.ANY)
     smem = pl.BlockSpec(memory_space=pltpu.SMEM)
@@ -194,8 +206,8 @@
 
 
 def attend_body(
-    old_block, lengths, meta, q, k, v, ok, ov, dk, dv, packet,
-    vq, vk, vv, vok, vov, scores, drafted, peak, total, acc, owner, live, sems,
+    old_block, lengths, meta, q, k, v, ok, ov, dks, dvs, packet,
+    vq, dk, dv, vk, vv, vok, vov, scores, drafted, peak, total, acc, owner, live, sems,
 ):
     requests, draft, width = vq.shape
     head_dim = vk.shape[2]
@@ -207,10 +219,16 @@
     rows = requests // insts
     inv_root = 1.0 / math.sqrt(head_dim)
     is_source = old_block[0] >= 0
-    first = meta[0]
-    shift = meta[1]
-    load_q = pltpu.make_async_copy(q, vq, sems.at[0])
-    load_q.start()
+    first = meta[insts]
+    shift = meta[insts + 1]
+    kv = pl.ds(pl.multiple_of(meta[insts + 2], head_dim), head_dim)
+    early = [
+        pltpu.make_async_copy(q, vq, sems.at[0]),
+        pltpu.make_async_copy(dks.at[:, :, kv], dk, sems.at[5]),
+        pltpu.make_async_copy(dvs.at[:, :, kv], dv, sems.at[6]),
+    ]
+    for load in early:
+        load.start()
     loads = [
         pltpu.make_async_copy(x, y, sems.at[1 + n])
         for n, (x, y) in enumerate(((k, vk), (ok, vok), (v, vv), (ov, vov)))
@@ -251,7 +269,8 @@
         return c
 
     lax.fori_loop(0, requests, reset, 0, unroll=4)
-    load_q.wait()
+    for load in early:
+        load.wait()
     pad = jnp.zeros((2 * half - draft, head_dim), dk.dtype)
     for a in range(rows):
         s = dot_t(q_of(first + a), jnp.concatenate([dk[a], pad], axis=0)) * inv_root
@@ -265,13 +284,15 @@
         loads[1].wait()
 
         def score(n, c):
+            found = []
             for u in range(UNROLL):
                 i = n * UNROLL + u
                 g = jnp.maximum(old_block[i], 0)
                 r = owner[g]
                 key = jnp.concatenate([vk[i], vok[i]], axis=0)
                 s = dot_t(q_of(r), key) * inv_root
-                s = jnp.where(place < live[g], s, masked)
+                found.append((i, r, jnp.where(place < live[g], s, masked)))
+            for i, r, s in found:
                 scores[i] = s
                 peak[r] = jnp.maximum(peak[r], s)
             return c
@@ -284,7 +305,7 @@
         acc[r] = jnp.zeros((qrows, head_dim), jnp.float32)
         return c
 
-    lax.fori_loop(0, requests, settle, 0, unroll=2)
+    lax.fori_loop(0, requests, settle, 0, unroll=SETTLE)
     for a in range(rows):
         w = jnp.exp(drafted[a] - peak[first + a])
         total[first + a] = w
@@ -300,12 +321,15 @@
         loads[3].wait()
 
         def gather(n, c):
+            found = []
             for u in range(UNROLL):
                 i = n * UNROLL + u
                 r = owner[jnp.maximum(old_block[i], 0)]
                 w = jnp.exp(scores[i] - peak[r])
                 value = jnp.concatenate([vv[i], vov[i]], axis=0)
                 out = jnp.dot(w.astype(vv.dtype), value, preferred_element_type=jnp.float32)
+                found.append((r, w, out))
+            for r, w, out in found:
                 total[r] += w
                 acc[r] += out
             return c
@@ -313,27 +337,27 @@
         lax.fori_loop(0, slots // UNROLL, gather, 0)
 
     def finish(d, c):
-        stat = jnp.zeros((qrows, head_dim), jnp.float32)
+        sums = jnp.zeros((qrows, head_dim), jnp.float32)
+        tops = jnp.zeros((qrows, head_dim), jnp.float32)
         for a in range(rows):
             r = d * rows + a
             l = jnp.sum(total[r], axis=1, keepdims=True)
-            seen = l > 0
-            safe = jnp.where(seen, l, 1.0)
-            packet[d, a * qrows : (a + 1) * qrows, :] = (acc[r] / safe).astype(packet.dtype)
-            level = jnp.where(seen, peak[r] + jnp.log(safe), masked)
-            hi = level.astype(jnp.bfloat16).astype(jnp.float32)
-            mid = (level - hi).astype(jnp.bfloat16).astype(jnp.float32)
-            low = level - hi - mid
-            stat = jnp.where(lane == 3 * a, hi, stat)
-            stat = jnp.where(lane == 3 * a + 1, mid, stat)
-            stat = jnp.where(lane == 3 * a + 2, low, stat)
+            scale = 1.0 / jnp.where(l > 0, l, 1.0)
+            packet[d, a * qrows : (a + 1) * qrows, :] = (acc[r] * scale).astype(packet.dtype)
+            sums = jnp.where(lane % rows == a, l, sums)
+            tops = jnp.where(lane % rows == a, peak[r], tops)
+        level = jnp.where(sums > 0, tops + jnp.log(jnp.where(sums > 0, sums, 1.0)), masked)
+        hi = level.astype(jnp.bfloat16).astype(jnp.float32)
+        mid = (level - hi).astype(jnp.bfloat16).astype(jnp.float32)
+        stat = jnp.where(lane < rows, hi, jnp.where(lane < 2 * rows, mid, level - hi - mid))
         packet[d, rows * qrows :, :] = stat.astype(packet.dtype)
         return c
 
     lax.fori_loop(0, insts, finish, 0)
 
 
-UNROLL = 4
+UNROLL = 16
+SETTLE = 16
 
 
 def attend(old_block, lengths, meta, queries, keys, values, other_k, other_v, dk, dv, insts):
@@ -348,10 +372,11 @@
     state = pltpu.VMEM((requests, qrows, head_dim), jnp.float32)
     return pl.pallas_call(
         attend_body,
-        in_specs=[smem] * 3 + [anyspace] * 5 + [vmem] * 2,
+        in_specs=[smem] * 3 + [anyspace] * 7,
         out_specs=vmem,
         out_shape=jax.ShapeDtypeStruct((insts, (rows + 1) * qrows, head_dim), bf16),
         scratch_shapes=[pltpu.VMEM(queries.shape, bf16)]
+        + [pltpu.VMEM((rows, draft, head_dim), bf16)] * 2
         + [pltpu.VMEM(keys.shape, bf16)] * 4
         + [
             pltpu.VMEM((keys.shape[0], qrows, head_dim), jnp.float32),
@@ -361,7 +386,7 @@
             state,
             pltpu.SMEM((TOTAL,), jnp.int32),
             pltpu.SMEM((TOTAL,), jnp.int32),
-            pltpu.SemaphoreType.DMA((5,)),
+            pltpu.SemaphoreType.DMA((7,)),
         ],
         name="attend",
     )(old_block, lengths, meta, queries, keys, values, other_k, other_v, dk, dv)
@@ -379,7 +404,7 @@
     lane = lax.broadcasted_iota(jnp.int32, (qrows, head_dim), 1)
     stats = [got[s, rows * qrows :, :].astype(jnp.float32) for s in range(insts)]
     for a in range(rows):
-        mine = (lane >= 3 * a) & (lane < 3 * a + 3)
+        mine = (lane % rows == a) & (lane < 3 * rows)
         level = [
             jnp.sum(jnp.where(mine, stat, 0.0), axis=1, keepdims=True) for stat in stats
         ]
@@ -418,8 +443,6 @@
     old_keys, old_values, old_block, new_slot, lengths, queries, draft_keys, draft_values
 ):
     insts = lax.axis_size("inst")
-    inst = lax.axis_index("inst")
-    me_head = lax.axis_index("head")
     _, entries, half, head_dim = old_keys.shape
     keys = old_keys.reshape(-1, half, head_dim)
     values = old_values.reshape(-1, half, head_dim)
@@ -430,7 +453,8 @@
     other_k = lax.ppermute(keys, "head", swap)
     other_v = lax.ppermute(values, "head", swap)
 
-    out_k, out_v = pack(old_block, new_slot, keys, values, inst, insts)
+    table = table_of(blocks // insts, rows, half, head_dim)
+    out_k, out_v = pack(old_block, new_slot, table, keys, values, insts)
     queries, out_k, out_v = lax.optimization_barrier((queries, out_k, out_v))
     shape = (blocks // insts, entries, half, head_dim)
     far = across(out_v[0])
@@ -438,12 +462,9 @@
     from_right = left(out_k[1])
     near = across(out_v[1])
 
-    kv_head = me_head // 2
-    dk = lax.dynamic_slice_in_dim(draft_keys, kv_head * head_dim, head_dim, 2)
-    dv = lax.dynamic_slice_in_dim(draft_values, kv_head * head_dim, head_dim, 2)
-    meta = jnp.stack([inst * rows, me_head % 2 * half])
     packet = attend(
-        old_block, lengths, meta, queries, keys, values, other_k, other_v, dk, dv, insts
+        old_block, lengths, table, queries, keys, values, other_k, other_v,
+        draft_keys, draft_values, insts,
     )
     packet, rest_k, rest_v = lax.optimization_barrier((packet, out_k[2:], out_v[2:]))
     moved_keys = move_keys(from_left, from_right, rest_k).reshape(shape)

time: 115 us -> 117 us (1.017)
  waiting for transfers between devices: 28.4 us -> 44.3 us
  starting transfers between devices: 45.7 us -> 35.3 us
  Pallas kernels: 25.1 us -> 22.4 us
  local copies, waits for them, and re-layouts: 6.47 us -> 5.07 us
    ppermute x3, waiting for transfers between devices: 21.9 us -> 31 us  [across(): lax.ppermute(x, 'inst', [(i, i ^ COLS) for i in range(lax.axis_size('inst...]
    all_to_all x2, starting transfers between devices: 18.8 us -> 14 us  [spread(): return lax.all_to_all(x, 'inst', split_axis=0, concat_axis=0, tiled=True)]
    ppermute x4, waiting for transfers between devices: 1.69 us -> 5.99 us  [right(): return lax.ppermute(x, 'inst', route)]
    all_to_all x2, waiting for transfers between devices: 0.01 us -> 2.81 us  [spread(): return lax.all_to_all(x, 'inst', split_axis=0, concat_axis=0, tiled=True)]
    ppermute x3, starting transfers between devices: 13.5 us -> 10.7 us  [across(): lax.ppermute(x, 'inst', [(i, i ^ COLS) for i in range(lax.axis_size('inst...]
    pallas_call x1, Pallas kernels: 8.32 us -> 5.57 us  [attend(): pl.pallas_call(attend_body, in_specs=[smem] * 3 + [anyspace] * 7, out_spe...]
    ppermute x4, starting transfers between devices: 10 us -> 8.16 us  [left(): return lax.ppermute(x, 'inst', route)]
    dynamic_slice x1 -> x0, local copies, waits for them, and re-layouts: 1.41 us -> none  [move_and_attend(): dv = lax.dynamic_slice_in_dim(draft_values, kv_head * head_dim, head_dim, 2)]
  transfers between devices with their start and end apart: 15 -> 15, of which waited for: 5 -> 6; matrix products, arithmetic and copies ran while one was open for 8% -> 6% of each run, Pallas kernels for 22% -> 20%
where the time goes in v1:
time: 117 us; the launch traced here: 115 us
  waiting for transfers between devices  44.3 us (38%)
  starting transfers between devices  35.3 us (30%)
  Pallas kernels  22.4 us (19%)
  other arithmetic  6.87 us (6%)
  local copies, waits for them, and re-layouts  5.07 us (4%)
    ppermute x3, waiting for transfers between devices, across(): lax.ppermute(x, 'inst', [(i, i ^ COLS) for i in range(lax.axis_size('inst...  31 us
    all_to_all x2, starting transfers between devices, spread(): return lax.all_to_all(x, 'inst', split_axis=0, concat_axis=0, tiled=True)  14 us
    ppermute x3, starting transfers between devices, across(): lax.ppermute(x, 'inst', [(i, i ^ COLS) for i in range(lax.axis_size('inst...  10.7 us
    pallas_call x3, Pallas kernels, vmem_call(): pl.pallas_call(body, in_specs=[vmem] * len(args), out_specs=[vmem] * len(...  9.61 us
    ppermute x4, starting transfers between devices, left(): return lax.ppermute(x, 'inst', route)  8.16 us
    ppermute x4, waiting for transfers between devices, right(): return lax.ppermute(x, 'inst', route)  5.99 us
    pallas_call x1, Pallas kernels, attend(): pl.pallas_call(attend_body, in_specs=[smem] * 3 + [anyspace] * 7, out_spe...  5.57 us
    unnamed x19, local copies, waits for them, and re-layouts  5.07 us
  transfers between devices with their start and end apart: 15, of which 6 were waited for; matrix products, arithmetic and copies ran while one was open for 6% of the time, Pallas kernels for 20%

profile of v1, /device:TPU:0, one launch (start us, length us, event | category | flops | bytes accessed | tf_op | source)
XLA Modules:
  0.0 114.8 jit_solution(9534615222968443124)
XLA Ops:
  0.6 0.1 collective-permute-start.2
  0.7 0.5 collective-permute-start.3
  1.2 0.6 compare_select_fusion.4.base.meta
  1.8 4.1 %pack.1 = (bf16[64,64,128]{2,1,0:T(8,128)(2,1)}, bf16[64,64,128]{2,1,0:T(8,128)(2,1)}, bf16[32,64,128]{2,1,0:T(8,128)(2,1)}, bf16[32,64,128]{2,1,0:T(8,128)(2,1)...) custom-call(s32[128]{0:T(128)} %old_block.3, ...), custom_call_target="tpu_custom_call" | custom-call | tf_op jit(solution)/shard_map/pack/pallas_call | solution.py:106
  6.0 5.4 %collective-permute-start.8 = (bf16[96,64,128]{2,1,0:T(8,128)(2,1)}, bf16[96,64,128]{2,1,0:T(8,128)(2,1)}, u32[]{:S(2)}, u32[]{:S(2)}) collective-permute-start(bf16[96,64,128]{2,1,0:T(8,128)(2,1)} %get-tuple-element.80), channel_id=1, source_target_pairs={{0,64},{16,80},{32,96},{48,112},{64,0},{80,16},{96,32},{112,48},{1... | collective-permute-start | bytes 4718600 | tf_op jit(solution)/shard_map/ppermute | solution.py:139
  11.4 0.0 collective-permute-start
  11.4 3.2 %collective-permute-start.1 = (bf16[64,64,128]{2,1,0:T(8,128)(2,1)}, bf16[64,64,128]{2,1,0:T(8,128)(2,1)}, u32[]{:S(2)}, u32[]{:S(2)}) collective-permute-start(bf16[64,64,128]{2,1,0:T(8,128)(2,1)} %get-tuple-element.60), channel_id=1, source_target_pairs={{16,0},{32,16},{48,32},{0,48},{80,64},{96,80},{112,96},{64,112},{1... | collective-permute-start | bytes 3145736 | tf_op jit(solution)/shard_map/ppermute | solution.py:135
  14.6 0.0 collective-permute-done.2.ok
  14.6 0.0 collective-permute-done.3.ov
  14.6 1.3 %copy-done.1 = bf16[128,64,128]{2,1,0:T(8,128)(2,1)} copy-done((bf16[128,64,128]{2,1,0:T(8,128)(2,1)}, bf16[128,64,128]{2,1,0:T(8,128)(2,1)S(1)}, u32[]{:S(2)}) %copy-start.1) | copy-done | bytes 2097176
  15.9 5.6 %attend.1 = bf16[8,576,128]{2,1,0:T(8,128)(2,1)} custom-call(s32[128]{0:T(128)} %old_block.3, s32[64]{0:T(128)} %lengths.1, s32[16]{0:T(128)} %compare_select_fusion.4.base.meta, bf16[64,16,512]{2,1,0:T(8,128)(2,1)} %q, bf16[128,64,128]{2,1,0:T(8,128)(2,1)} %bitcast.13, bf16[128,64,128]{2,1,0:T(8,128)(2,1)} %bitcast.16, bf16[128,64,128]{2,1,0:T(8,128)(2,1)} %copy-done.1, ...), custom_call_target="tpu_custom_call" | custom-call | tf_op jit(solution)/shard_map/attend/pallas_call | solution.py:373
  21.5 9.0 %all-to-all-start = ((bf16[8,576,128]{2,1,0:T(8,128)(2,1)}), bf16[8,576,128]{2,1,0:T(8,128)(2,1)S(1)}, u32[]{:S(2)}, u32[]{:S(2)}) async-start(bf16[8,576,128]{2,1,0:T(8,128)(2,1)} %attend.1), calls=%async_computation | async-start | bytes 2359296 | tf_op jit(solution)/shard_map/all_to_all | solution.py:439
  30.5 25.9 %collective-permute-done.8.far = bf16[96,64,128]{2,1,0:T(8,128)(2,1)} collective-permute-done((bf16[96,64,128]{2,1,0:T(8,128)(2,1)}, bf16[96,64,128]{2,1,0:T(8,128)(2,1)}, u32[]{:S(2)}, u32[]{:S(2)}) %collective-permute-start.8) | collective-permute-done | bytes 1572896 | tf_op jit(solution)/shard_map/ppermute | solution.py:139
  56.4 3.4 %shard_map.104 = (bf16[32,64,128]{2,1,0:T(8,128)(2,1)}, bf16[32,64,128]{2,1,0:T(8,128)(2,1)}, bf16[16,64,128]{2,1,0:T(8,128)(2,1)}, bf16[16,64,128]{2,1,0:T(8,128)(2,1)}) custom-call(bf16[96,64,128]{2,1,0:T(8,128)(2,1)} %collective-permute-done.8.far, bf16[32,64,128]{2,1,0:T(8,128)(2,1)} %get-tuple-element.81.v2n, ...), custom_call_target="tpu_custom_call" | custom-call | tf_op jit(solution)/shard_map/pallas_call | solution.py:144
  59.8 1.8 %collective-permute-start.9 = (bf16[32,64,128]{2,1,0:T(8,128)(2,1)}, bf16[32,64,128]{2,1,0:T(8,128)(2,1)S(1)}, u32[]{:S(2)}, u32[]{:S(2)}) collective-permute-start(bf16[32,64,128]{2,1,0:T(8,128)(2,1)} %get-tuple-element.86), channel_id=1, source_target_pairs={{0,16},{16,32},{32,48},{48,0},{64,80},{80,96},{96,112},{112,64},{1... | collective-permute-start | bytes 1572872 | tf_op jit(solution)/shard_map/ppermute | solution.py:129
  61.6 1.4 %collective-permute-start.10 = (bf16[32,64,128]{2,1,0:T(8,128)(2,1)}, bf16[32,64,128]{2,1,0:T(8,128)(2,1)S(1)}, u32[]{:S(2)}, u32[]{:S(2)}) collective-permute-start(bf16[32,64,128]{2,1,0:T(8,128)(2,1)} %get-tuple-element.87), channel_id=1, source_target_pairs={{16,0},{32,16},{48,32},{0,48},{80,64},{96,80},{112,96},{64,112},{1... | collective-permute-start | bytes 1572872 | tf_op jit(solution)/shard_map/ppermute | solution.py:135
  63.0 0.0 collective-permute-done.from_left
  63.0 0.0 collective-permute-done.1.from_right
  63.0 1.0 copy-done.6
  64.0 4.0 %shard_map.103 = (bf16[32,64,128]{2,1,0:T(8,128)(2,1)}, bf16[32,64,128]{2,1,0:T(8,128)(2,1)}, bf16[32,64,128]{2,1,0:T(8,128)(2,1)}, bf16[32,64,128]{2,1,0:T(8,128)(2,1)}) custom-call(bf16[64,64,128]{2,1,0:T(8,128)(2,1)} %copy-done.6, bf16[64,64,128]{2,1,0:T(8,128)(2,1)} %collective-permute-done.1.from_right, bf16[32,64,128]{2,1,0:T(8,128)(2,1)} %get-tuple-element.70.k1n, ...), custom_call_target="tpu_custom_call" | custom-call | tf_op jit(solution)/shard_map/pallas_call | solution.py:144
  68.0 0.0 collective-permute-start.5
  68.0 6.0 %collective-permute-done.9.from_left = bf16[32,64,128]{2,1,0:T(8,128)(2,1)S(1)} collective-permute-done((bf16[32,64,128]{2,1,0:T(8,128)(2,1)}, bf16[32,64,128]{2,1,0:T(8,128)(2,1)S(1)}, u32[]{:S(2)}, u32[]{:S(2)}) %collective-permute-start.9) | collective-permute-done | bytes 524320 | tf_op jit(solution)/shard_map/ppermute | solution.py:129
  74.0 2.6 %collective-permute-done.10.from_right = bf16[32,64,128]{2,1,0:T(8,128)(2,1)S(1)} collective-permute-done((bf16[32,64,128]{2,1,0:T(8,128)(2,1)}, bf16[32,64,128]{2,1,0:T(8,128)(2,1)S(1)}, u32[]{:S(2)}, u32[]{:S(2)}) %collective-permute-start.10) | collective-permute-done | bytes 524320 | tf_op jit(solution)/shard_map/ppermute | solution.py:135
  76.6 0.8 copy-done.4
  77.4 2.3 %shard_map.105 = (bf16[16,64,128]{2,1,0:T(8,128)(2,1)}, bf16[16,64,128]{2,1,0:T(8,128)(2,1)}) custom-call(bf16[16,64,128]{2,1,0:T(8,128)(2,1)} %get-tuple-element.84.low, bf16[16,64,128]{2,1,0:T(8,128)(2,1)} %get-tuple-element.85.high, bf16[32,64,128]{2,1,0:T(8,128)(2,1)} %copy-done.2, bf16[32,64,128]{2,1,0:T(8,128)(2,1)} %copy-done.4), custom_call_target="tpu_custom_call" | custom-call | tf_op jit(solution)/shard_map/pallas_call | solution.py:144
  79.7 0.0 collective-permute-start.11
  79.7 2.6 %collective-permute-start.7 = (bf16[32,64,128]{2,1,0:T(8,128)(2,1)}, bf16[32,64,128]{2,1,0:T(8,128)(2,1)}, u32[]{:S(2)}, u32[]{:S(2)}) collective-permute-start(bf16[32,64,128]{2,1,0:T(8,128)(2,1)} %get-tuple-element.79), channel_id=1, source_target_pairs={{0,64},{16,80},{32,96},{48,112},{64,0},{80,16},{96,32},{112,48},{1... | collective-permute-start | bytes 1572872 | tf_op jit(solution)/shard_map/ppermute | solution.py:139
  82.3 3.5 %collective-permute-start.12 = (bf16[16,64,128]{2,1,0:T(8,128)(2,1)}, bf16[16,64,128]{2,1,0:T(8,128)(2,1)}, u32[]{:S(2)}, u32[]{:S(2)}) collective-permute-start(bf16[16,64,128]{2,1,0:T(8,128)(2,1)} %get-tuple-element.89), channel_id=1, source_target_pairs={{16,0},{32,16},{48,32},{0,48},{80,64},{96,80},{112,96},{64,112},{1... | collective-permute-start | bytes 786440 | tf_op jit(solution)/shard_map/ppermute | solution.py:135
  85.8 0.0 collective-permute-start.4
  85.8 1.9 %collective-permute-done.5 = bf16[32,64,128]{2,1,0:T(8,128)(2,1)S(1)} collective-permute-done((bf16[32,64,128]{2,1,0:T(8,128)(2,1)}, bf16[32,64,128]{2,1,0:T(8,128)(2,1)S(1)}, u32[]{:S(2)}, u32[]{:S(2)}) %collective-permute-start.5) | collective-permute-done | bytes 524320 | tf_op jit(solution)/shard_map/ppermute | solution.py:135
  87.8 1.2 %add.58 = bf16[32,64,128]{2,1,0:T(8,128)(2,1)S(1)} add(bf16[32,64,128]{2,1,0:T(8,128)(2,1)} %get-tuple-element.76, bf16[32,64,128]{2,1,0:T(8,128)(2,1)S(1)} %collective-permute-done.5) | non-fusion elementwise | flops 262144 | bytes 1572864 | tf_op jit(solution)/shard_map/add | solution.py:167
  89.0 0.0 copy-start.5
  89.0 0.0 copy-start.3
  89.0 2.6 %collective-permute-start.6 = (bf16[32,64,128]{2,1,0:T(8,128)(2,1)S(1)}, bf16[32,64,128]{2,1,0:T(8,128)(2,1)}, u32[]{:S(2)}, u32[]{:S(2)}) collective-permute-start(bf16[32,64,128]{2,1,0:T(8,128)(2,1)S(1)} %add.58), channel_id=1, source_target_pairs={{0,64},{16,80},{32,96},{48,112},{64,0},{80,16},{96,32},{112,48},{1... | collective-permute-start | bytes 1572872 | tf_op jit(solution)/shard_map/ppermute | solution.py:139
  91.7 0.0 all-to-all-done.got
  91.7 1.0 copy-done
  92.7 3.1 %join.1 = bf16[8,8,16,512]{3,2,1,0:T(8,128)(2,1)} custom-call(bf16[8,576,128]{2,1,0:T(8,128)(2,1)} %copy-done), custom_call_target="tpu_custom_call" | custom-call | tf_op jit(solution)/shard_map/join/pallas_call | solution.py:429
  95.8 5.0 %all-to-all-start.1 = ((bf16[8,8,16,512]{3,2,1,0:T(8,128)(2,1)}), bf16[8,8,16,512]{3,2,1,0:T(8,128)(2,1)S(1)}, u32[]{:S(2)}, u32[]{:S(2)}) async-start(bf16[8,8,16,512]{3,2,1,0:T(8,128)(2,1)} %join.1), calls=%async_computation.1 | async-start | bytes 2097152 | tf_op jit(solution)/shard_map/all_to_all | solution.py:439
  100.8 0.0 collective-permute-done.11
  100.9 0.0 collective-permute-done.12
  100.9 1.0 slice_add_fusion
  101.9 0.0 collective-permute-done.7
  101.9 1.9 %fusion = bf16[32,1,64,128]{3,2,1,0:T(8,128)(2,1)} fusion(bf16[16,64,128]{2,1,0:T(8,128)(2,1)S(1)} %slice_add_fusion, bf16[16,64,128]{2,1,0:T(8,128)(2,1)S(1)} %slice_add_fusion.1, bf16[32,64,128]{2,1,0:T(8,128)(2,1)S(1)} %copy-done.7, bf16[32,64,128]{2,1,0:T(8,128)(2,1)} %collective-permute-done.7), kind=kLoop, calls=%fused_computation.1 | loop fusion | flops 786432 | bytes 2097152
  103.8 0.0 collective-permute-done.4
  103.8 5.1 %collective-permute-done.6 = bf16[32,64,128]{2,1,0:T(8,128)(2,1)} collective-permute-done((bf16[32,64,128]{2,1,0:T(8,128)(2,1)S(1)}, bf16[32,64,128]{2,1,0:T(8,128)(2,1)}, u32[]{:S(2)}, u32[]{:S(2)}) %collective-permute-start.6) | collective-permute-done | bytes 524320 | tf_op jit(solution)/shard_map/ppermute | solution.py:139
  108.9 2.1 %add_bitcast_fusion = bf16[32,1,64,128]{3,2,1,0:T(8,128)(2,1)} fusion(bf16[32,64,128]{2,1,0:T(8,128)(2,1)} %collective-permute-done.6, bf16[32,64,128]{2,1,0:T(8,128)(2,1)S(1)} %copy-done.8, bf16[32,64,128]{2,1,0:T(8,128)(2,1)} %collective-permute-done.4), kind=kLoop, calls=%fused_computation.2 | loop fusion | flops 524288 | bytes 2097152
  111.0 2.8 %all-to-all-done.1 = bf16[8,8,16,512]{3,2,1,0:T(8,128)(2,1)S(1)} async-done(((bf16[8,8,16,512]{3,2,1,0:T(8,128)(2,1)}), bf16[8,8,16,512]{3,2,1,0:T(8,128)(2,1)S(1)}, u32[]{:S(2)}, u32[]{:S(2)}) %all-to-all-start.1) | async-done | bytes 1048608 | tf_op jit(solution)/shard_map/all_to_all | solution.py:439
  113.8 1.0 copy.14
  (13 shorter events, 0.1 us)
Async XLA Ops:
  0.6 14.0 %collective-permute-start.2 = (bf16[128,64,128]{2,1,0:T(8,128)(2,1)}, bf16[128,64,128]{2,1,0:T(8,128)(2,1)S(1)}, u32[]{:S(2)}, u32[]{:S(2)}) collective-permute-start(bf16[128,64,128]{2,1,0:T(8,128)(2,1)} %bitcast.11), channel_id=1, source_target_pairs={{0,1},{1,0},{2,3},{3,2},{4,5},{5,4},{6,7},{7,6},{8,9},{9,8},{10,11... | collective-permute-start | bytes 6291464 | tf_op jit(solution)/shard_map/ppermute | solution.py:453
  0.7 13.9 %collective-permute-start.3 = (bf16[128,64,128]{2,1,0:T(8,128)(2,1)}, bf16[128,64,128]{2,1,0:T(8,128)(2,1)}, u32[]{:S(2)}, u32[]{:S(2)}) collective-permute-start(bf16[128,64,128]{2,1,0:T(8,128)(2,1)} %bitcast.14), channel_id=1, source_target_pairs={{0,1},{1,0},{2,3},{3,2},{4,5},{5,4},{6,7},{7,6},{8,9},{9,8},{10,11... | collective-permute-start | bytes 6291464 | tf_op jit(solution)/shard_map/ppermute | solution.py:454
  6.0 50.5 %collective-permute-start.8 = (bf16[96,64,128]{2,1,0:T(8,128)(2,1)}, bf16[96,64,128]{2,1,0:T(8,128)(2,1)}, u32[]{:S(2)}, u32[]{:S(2)}) collective-permute-start(bf16[96,64,128]{2,1,0:T(8,128)(2,1)} %get-tuple-element.80), channel_id=1, source_target_pairs={{0,64},{16,80},{32,96},{48,112},{64,0},{80,16},{96,32},{112,48},{1... | collective-permute-start | bytes 4718600 | tf_op jit(solution)/shard_map/ppermute | solution.py:139
  11.4 51.6 %collective-permute-start = (bf16[64,64,128]{2,1,0:T(8,128)(2,1)}, bf16[64,64,128]{2,1,0:T(8,128)(2,1)S(1)}, u32[]{:S(2)}, u32[]{:S(2)}) collective-permute-start(bf16[64,64,128]{2,1,0:T(8,128)(2,1)} %get-tuple-element.59), channel_id=1, source_target_pairs={{0,16},{16,32},{32,48},{48,0},{64,80},{80,96},{96,112},{112,64},{1... | collective-permute-start | bytes 3145736 | tf_op jit(solution)/shard_map/ppermute | solution.py:129
  11.4 51.6 %collective-permute-start.1 = (bf16[64,64,128]{2,1,0:T(8,128)(2,1)}, bf16[64,64,128]{2,1,0:T(8,128)(2,1)}, u32[]{:S(2)}, u32[]{:S(2)}) collective-permute-start(bf16[64,64,128]{2,1,0:T(8,128)(2,1)} %get-tuple-element.60), channel_id=1, source_target_pairs={{16,0},{32,16},{48,32},{0,48},{80,64},{96,80},{112,96},{64,112},{1... | collective-permute-start | bytes 3145736 | tf_op jit(solution)/shard_map/ppermute | solution.py:135
  14.6 1.3 %copy-start.1 = (bf16[128,64,128]{2,1,0:T(8,128)(2,1)}, bf16[128,64,128]{2,1,0:T(8,128)(2,1)S(1)}, u32[]{:S(2)}) copy-start(bf16[128,64,128]{2,1,0:T(8,128)(2,1)S(1)} %collective-permute-done.2.ok) | copy-start | bytes 6291460
  21.5 70.2 %all-to-all-start = ((bf16[8,576,128]{2,1,0:T(8,128)(2,1)}), bf16[8,576,128]{2,1,0:T(8,128)(2,1)S(1)}, u32[]{:S(2)}, u32[]{:S(2)}) async-start(bf16[8,576,128]{2,1,0:T(8,128)(2,1)} %attend.1), calls=%async_computation | async-start | bytes 2359296 | tf_op jit(solution)/shard_map/all_to_all | solution.py:439
  59.8 14.2 %collective-permute-start.9 = (bf16[32,64,128]{2,1,0:T(8,128)(2,1)}, bf16[32,64,128]{2,1,0:T(8,128)(2,1)S(1)}, u32[]{:S(2)}, u32[]{:S(2)}) collective-permute-start(bf16[32,64,128]{2,1,0:T(8,128)(2,1)} %get-tuple-element.86), channel_id=1, source_target_pairs={{0,16},{16,32},{32,48},{48,0},{64,80},{80,96},{96,112},{112,64},{1... | collective-permute-start | bytes 1572872 | tf_op jit(solution)/shard_map/ppermute | solution.py:129
  61.6 15.0 %collective-permute-start.10 = (bf16[32,64,128]{2,1,0:T(8,128)(2,1)}, bf16[32,64,128]{2,1,0:T(8,128)(2,1)S(1)}, u32[]{:S(2)}, u32[]{:S(2)}) collective-permute-start(bf16[32,64,128]{2,1,0:T(8,128)(2,1)} %get-tuple-element.87), channel_id=1, source_target_pairs={{16,0},{32,16},{48,32},{0,48},{80,64},{96,80},{112,96},{64,112},{1... | collective-permute-start | bytes 1572872 | tf_op jit(solution)/shard_map/ppermute | solution.py:135
  63.0 1.0 copy-start.6
  68.0 19.8 %collective-permute-start.5 = (bf16[32,64,128]{2,1,0:T(8,128)(2,1)}, bf16[32,64,128]{2,1,0:T(8,128)(2,1)S(1)}, u32[]{:S(2)}, u32[]{:S(2)}) collective-permute-start(bf16[32,64,128]{2,1,0:T(8,128)(2,1)} %get-tuple-element.77), channel_id=1, source_target_pairs={{16,0},{32,16},{48,32},{0,48},{80,64},{96,80},{112,96},{64,112},{1... | collective-permute-start | bytes 1572872 | tf_op jit(solution)/shard_map/ppermute | solution.py:135
  74.0 2.7 %copy-start.2 = (bf16[32,64,128]{2,1,0:T(8,128)(2,1)}, bf16[32,64,128]{2,1,0:T(8,128)(2,1)S(1)}, u32[]{:S(2)}) copy-start(bf16[32,64,128]{2,1,0:T(8,128)(2,1)S(1)} %collective-permute-done.9.from_left) | copy-start | bytes 1572868
  76.6 0.8 copy-start.4
  79.7 21.1 %collective-permute-start.11 = (bf16[16,64,128]{2,1,0:T(8,128)(2,1)}, bf16[16,64,128]{2,1,0:T(8,128)(2,1)S(1)}, u32[]{:S(2)}, u32[]{:S(2)}) collective-permute-start(bf16[16,64,128]{2,1,0:T(8,128)(2,1)} %get-tuple-element.88), channel_id=1, source_target_pairs={{0,16},{16,32},{32,48},{48,0},{64,80},{80,96},{96,112},{112,64},{1... | collective-permute-start | bytes 786440 | tf_op jit(solution)/shard_map/ppermute | solution.py:129
  79.7 22.2 %collective-permute-start.7 = (bf16[32,64,128]{2,1,0:T(8,128)(2,1)}, bf16[32,64,128]{2,1,0:T(8,128)(2,1)}, u32[]{:S(2)}, u32[]{:S(2)}) collective-permute-start(bf16[32,64,128]{2,1,0:T(8,128)(2,1)} %get-tuple-element.79), channel_id=1, source_target_pairs={{0,64},{16,80},{32,96},{48,112},{64,0},{80,16},{96,32},{112,48},{1... | collective-permute-start | bytes 1572872 | tf_op jit(solution)/shard_map/ppermute | solution.py:139
  82.3 18.5 %collective-permute-start.12 = (bf16[16,64,128]{2,1,0:T(8,128)(2,1)}, bf16[16,64,128]{2,1,0:T(8,128)(2,1)}, u32[]{:S(2)}, u32[]{:S(2)}) collective-permute-start(bf16[16,64,128]{2,1,0:T(8,128)(2,1)} %get-tuple-element.89), channel_id=1, source_target_pairs={{16,0},{32,16},{48,32},{0,48},{80,64},{96,80},{112,96},{64,112},{1... | collective-permute-start | bytes 786440 | tf_op jit(solution)/shard_map/ppermute | solution.py:135
  85.8 18.0 %collective-permute-start.4 = (bf16[32,64,128]{2,1,0:T(8,128)(2,1)}, bf16[32,64,128]{2,1,0:T(8,128)(2,1)}, u32[]{:S(2)}, u32[]{:S(2)}) collective-permute-start(bf16[32,64,128]{2,1,0:T(8,128)(2,1)} %get-tuple-element.75), channel_id=1, source_target_pairs={{0,16},{16,32},{32,48},{48,0},{64,80},{80,96},{96,112},{112,64},{1... | collective-permute-start | bytes 1572872 | tf_op jit(solution)/shard_map/ppermute | solution.py:129
  89.0 11.8 %copy-start.5 = (bf16[32,64,128]{2,1,0:T(8,128)(2,1)S(1)}, bf16[32,64,128]{2,1,0:T(8,128)(2,1)}, u32[]{:S(2)}) copy-start(bf16[32,64,128]{2,1,0:T(8,128)(2,1)} %copy-done.4) | copy-start | bytes 1572868
  89.0 11.8 %copy-start.3 = (bf16[32,64,128]{2,1,0:T(8,128)(2,1)S(1)}, bf16[32,64,128]{2,1,0:T(8,128)(2,1)}, u32[]{:S(2)}) copy-start(bf16[32,64,128]{2,1,0:T(8,128)(2,1)} %copy-done.2) | copy-start | bytes 1572868
  89.0 19.9 %collective-permute-start.6 = (bf16[32,64,128]{2,1,0:T(8,128)(2,1)S(1)}, bf16[32,64,128]{2,1,0:T(8,128)(2,1)}, u32[]{:S(2)}, u32[]{:S(2)}) collective-permute-start(bf16[32,64,128]{2,1,0:T(8,128)(2,1)S(1)} %add.58), channel_id=1, source_target_pairs={{0,64},{16,80},{32,96},{48,112},{64,0},{80,16},{96,32},{112,48},{1... | collective-permute-start | bytes 1572872 | tf_op jit(solution)/shard_map/ppermute | solution.py:139
  91.7 1.0 copy-start
  95.8 6.1 %copy-start.7 = (bf16[32,64,128]{2,1,0:T(8,128)(2,1)S(1)}, bf16[32,64,128]{2,1,0:T(8,128)(2,1)}, u32[]{:S(2)}) copy-start(bf16[32,64,128]{2,1,0:T(8,128)(2,1)} %get-tuple-element.78) | copy-start | bytes 1572868
  95.8 18.0 %all-to-all-start.1 = ((bf16[8,8,16,512]{3,2,1,0:T(8,128)(2,1)}), bf16[8,8,16,512]{3,2,1,0:T(8,128)(2,1)S(1)}, u32[]{:S(2)}, u32[]{:S(2)}) async-start(bf16[8,8,16,512]{3,2,1,0:T(8,128)(2,1)} %join.1), calls=%async_computation.1 | async-start | bytes 2097152 | tf_op jit(solution)/shard_map/all_to_all | solution.py:439
  100.8 8.1 %copy-start.8 = (bf16[32,64,128]{2,1,0:T(8,128)(2,1)S(1)}, bf16[32,64,128]{2,1,0:T(8,128)(2,1)}, u32[]{:S(2)}) copy-start(bf16[32,64,128]{2,1,0:T(8,128)(2,1)} %get-tuple-element.74) | copy-start | bytes 1572868

commit v2 on v1

--- a/solution.py
+++ b/solution.py
@@ -13,10 +13,8 @@
 
 
 COLS = 4
-
-
 GROUPS_K = ((4, 3), (5, 6), (2,), (7,), (0,), (1,))
-GROUPS_V = ((5, 3, 7), (1,), (4,), (2,), (6,), (0,))
+GROUPS_V = ((5,), (3, 7), (1,), (4,), (2,), (6,), (0,))
 
 
 def pack_body(old_block, new_slot, base, keys, values, *rest):
@@ -139,66 +137,75 @@
     return lax.ppermute(x, "inst", [(i, i ^ COLS) for i in range(lax.axis_size("inst"))])
 
 
-def vmem_call(body, outs, *args):
-    vmem = pl.BlockSpec(memory_space=pltpu.VMEM)
+def add_call(sums, split=None):
+    per = sums[0][0][0].shape[0]
+    tail = sums[0][0][0].shape[1:]
+    step = per // 4
+    steps = per // step
+    args = [x for terms in sums for x, _ in terms]
+    where = [
+        pl.BlockSpec((step,) + tail, lambda i, at=first // step: (i + at, 0, 0))
+        for terms in sums
+        for _, first in terms
+    ]
+    if split:
+        args += split
+        where += [
+            pl.BlockSpec((step,) + tail, lambda i: (jnp.minimum(i, steps // 2 - 1), 0, 0)),
+            pl.BlockSpec((step,) + tail, lambda i: (jnp.maximum(i - steps // 2, 0), 0, 0)),
+        ]
+
+    def body(*refs):
+        i = pl.program_id(0)
+        outs = refs[len(args) :]
+        at = 0
+        for terms, out in zip(sums, outs):
+            value = refs[at][...]
+            for n in range(1, len(terms)):
+                value = value + refs[at + n][...]
+            at += len(terms)
+            out[...] = value
+        if split:
+
+            @pl.when(i < steps // 2)
+            def _():
+                outs[0][...] += refs[at][...]
+
+            @pl.when(i >= steps // 2)
+            def _():
+                outs[1][...] += refs[at + 1][...]
+
     return pl.pallas_call(
         body,
-        in_specs=[vmem] * len(args),
-        out_specs=[vmem] * len(outs),
-        out_shape=[jax.ShapeDtypeStruct(shape, args[0].dtype) for shape in outs],
+        grid=(steps,),
+        in_specs=where,
+        out_specs=[pl.BlockSpec((step,) + tail, lambda i: (i, 0, 0))] * len(sums),
+        out_shape=[jax.ShapeDtypeStruct((per,) + tail, args[0].dtype)] * len(sums),
     )(*args)
 
 
-def merge_keys_body(from_left, from_right, k1n, k3f, k0n, k0f, o_right, o_left, near, cross):
+def move_keys(from_left, from_right, groups):
+    k1n, k3f, k0n, k0f = groups
     per = k1n.shape[0]
-    o_right[...] = k1n[...] + from_left[:per]
-    o_left[...] = k3f[...] + from_right[:per]
-    near[...] = k0n[...] + from_right[per:]
-    cross[...] = k0f[...] + from_left[per:]
-
-
-def move_keys(from_left, from_right, groups):
-    piece = groups[0].shape
-    o_right, o_left, near, cross = vmem_call(
-        merge_keys_body, [piece] * 4, from_left, from_right, *groups
+    o_right, o_left = add_call([[(k1n, 0), (from_left, 0)], [(k3f, 0), (from_right, 0)]])
+    a2 = right(o_right)
+    b2 = left(o_left)
+    crossed = across(k0f + from_left[per:] + b2)
+    return k0n + from_right[per:] + a2 + crossed
+
+
+def move_values(got2, got, y0, groups):
+    v2n, v1n, v3n, v0n = groups
+    per = v1n.shape[0]
+    cut = per // 2
+    from_left = right(v2n[:cut] + got2[:cut])
+    from_right = left(v2n[cut:] + got2[cut:])
+    o_right, o_left = add_call(
+        [[(v1n, 0), (got, 0)], [(v3n, 0), (got, per)]], [from_left, from_right]
     )
     a2 = right(o_right)
     b2 = left(o_left)
-    crossed = across(cross + b2)
-    return near + a2 + crossed
-
-
-def merge_values_body(far, v2n, v1n, v3n, o_right, o_left, low, high):
-    per = v1n.shape[0]
-    cut = per // 2
-    o_right[:cut] = v2n[:cut] + far[:cut]
-    o_left[:cut] = v2n[cut:] + far[cut:per]
-    low[...] = v1n[:cut] + far[per : per + cut]
-    o_right[cut:] = v1n[cut:] + far[per + cut : 2 * per]
-    o_left[cut:] = v3n[:cut] + far[2 * per : 2 * per + cut]
-    high[...] = v3n[cut:] + far[2 * per + cut :]
-
-
-def second_body(low, high, from_left, from_right, o_right, o_left):
-    cut = low.shape[0]
-    o_right[...] = low[...] + from_left[:cut]
-    o_left[...] = high[...] + from_right[:cut]
-
-
-def move_values(got, y0, groups):
-    v2n, v1n, v3n, v0n = groups
-    cut = v1n.shape[0] // 2
-    piece = v1n.shape
-    part = (cut,) + piece[1:]
-    o_right, o_left, low, high = vmem_call(
-        merge_values_body, [piece, piece, part, part], got, v2n, v1n, v3n
-    )
-    from_left = right(o_right)
-    from_right = left(o_left)
-    o_right, o_left = vmem_call(second_body, [part, part], low, high, from_left, from_right)
-    e_lo = right(o_right)
-    g_hi = left(o_left)
-    return v0n + y0 + jnp.concatenate([e_lo + from_right[cut:], from_left[cut:] + g_hi])
+    return v0n + y0 + a2 + b2
 
 
 def dot_t(x, y):
@@ -457,18 +464,18 @@
     out_k, out_v = pack(old_block, new_slot, table, keys, values, insts)
     queries, out_k, out_v = lax.optimization_barrier((queries, out_k, out_v))
     shape = (blocks // insts, entries, half, head_dim)
-    far = across(out_v[0])
+    far2 = across(out_v[0])
     from_left = right(out_k[0])
     from_right = left(out_k[1])
-    near = across(out_v[1])
-
+    far = across(out_v[1])
+    near = across(out_v[2])
     packet = attend(
         old_block, lengths, table, queries, keys, values, other_k, other_v,
         draft_keys, draft_values, insts,
     )
-    packet, rest_k, rest_v = lax.optimization_barrier((packet, out_k[2:], out_v[2:]))
+    packet, rest_k, rest_v = lax.optimization_barrier((packet, out_k[2:], out_v[3:]))
     moved_keys = move_keys(from_left, from_right, rest_k).reshape(shape)
-    moved_values = move_values(far, near, rest_v).reshape(shape)
+    moved_values = move_values(far2, far, near, rest_v).reshape(shape)
     got = spread(packet)
     mine = join(got, rows, queries.shape[1], queries.shape[2])
     attended = spread(mine).reshape(queries.shape)

time: 117 us -> 114 us (0.974)
  starting transfers between devices: 35.3 us -> 40.2 us
  waiting for transfers between devices: 44.3 us -> 40.4 us
  local copies, waits for them, and re-layouts: 5.07 us -> 2.72 us
  Pallas kernels: 22.4 us -> 20.4 us
    ppermute x4, waiting for transfers between devices: 5.99 us -> 21 us  [right(): return lax.ppermute(x, 'inst', route)]
    ppermute x3 -> x4, waiting for transfers between devices: 31 us -> 16.4 us  [across(): lax.ppermute(x, 'inst', [(i, i ^ COLS) for i in range(lax.axis_size('inst...]
    all_to_all x2, starting transfers between devices: 14 us -> 19.7 us  [spread(): return lax.all_to_all(x, 'inst', split_axis=0, concat_axis=0, tiled=True)]
    all_to_all x2, waiting for transfers between devices: 2.81 us -> 0.01 us  [spread(): return lax.all_to_all(x, 'inst', split_axis=0, concat_axis=0, tiled=True)]
    unnamed x19 -> x17, local copies, waits for them, and re-layouts: 5.07 us -> 2.72 us
    pallas_call x3 -> x2, Pallas kernels: 9.61 us -> 7.61 us  [add_call(): pl.pallas_call(body, grid=(steps,), in_specs=where, out_specs=[pl.BlockSp...]
    ppermute x4, waiting for transfers between devices: 4.59 us -> 3.12 us  [left(): return lax.ppermute(x, 'inst', route)]
    add x3 -> x2, other arithmetic: 2.27 us -> 2.79 us  [the longest x1 1.55 us: move_keys(): crossed = across(k0f + from_left[per:] + b2)]
  transfers between devices with their start and end apart: 15 -> 16, of which waited for: 6 -> 7; matrix products, arithmetic and copies ran while one was open for 6% -> 7% of each run, Pallas kernels for 20% -> 18%
where the time goes in v2:
time: 114 us; the launch traced here: 112 us
  waiting for transfers between devices  40.4 us (35%)
  starting transfers between devices  40.2 us (35%)
  Pallas kernels  20.4 us (18%)
  other arithmetic  7.41 us (6%)
  local copies, waits for them, and re-layouts  2.72 us (2%)
    ppermute x4, waiting for transfers between devices, right(): return lax.ppermute(x, 'inst', route)  21 us
    all_to_all x2, starting transfers between devices, spread(): return lax.all_to_all(x, 'inst', split_axis=0, concat_axis=0, tiled=True)  19.7 us
    ppermute x4, waiting for transfers between devices, across(): lax.ppermute(x, 'inst', [(i, i ^ COLS) for i in range(lax.axis_size('inst...  16.4 us
    ppermute x4, starting transfers between devices, across(): lax.ppermute(x, 'inst', [(i, i ^ COLS) for i in range(lax.axis_size('inst...  10.6 us
    ppermute x4, starting transfers between devices, left(): return lax.ppermute(x, 'inst', route)  8.5 us
    pallas_call x2, Pallas kernels, add_call(): pl.pallas_call(body, grid=(steps,), in_specs=where, out_specs=[pl.BlockSp...  7.61 us
    pallas_call x1, Pallas kernels, attend(): pl.pallas_call(attend_body, in_specs=[smem] * 3 + [anyspace] * 7, out_spe...  5.51 us
    pallas_call x1, Pallas kernels, pack(): pl.pallas_call(pack_body, in_specs=[smem, smem, smem, anyspace, anyspace]...  4.16 us
  transfers between devices with their start and end apart: 16, of which 7 were waited for; matrix products, arithmetic and copies ran while one was open for 7% of the time, Pallas kernels for 18%

profile of v2, /device:TPU:0, one launch (start us, length us, event | category | flops | bytes accessed | tf_op | source)
XLA Modules:
  0.0 111.9 jit_solution(11801867979436189306)
XLA Ops:
  0.6 0.1 collective-permute-start
  0.7 0.5 collective-permute-start.1
  1.2 0.6 compare_select_fusion.4.base.meta
  1.8 4.2 %pack.1 = (bf16[64,64,128]{2,1,0:T(8,128)(2,1)}, bf16[64,64,128]{2,1,0:T(8,128)(2,1)}, bf16[32,64,128]{2,1,0:T(8,128)(2,1)}, bf16[32,64,128]{2,1,0:T(8,128)(2,1)...) custom-call(s32[128]{0:T(128)} %old_block.3, ...), custom_call_target="tpu_custom_call" | custom-call | tf_op jit(solution)/shard_map/pack/pallas_call | solution.py:104
  6.0 2.9 %collective-permute-start.2 = (bf16[64,64,128]{2,1,0:T(8,128)(2,1)}, bf16[64,64,128]{2,1,0:T(8,128)(2,1)S(1)}, u32[]{:S(2)}, u32[]{:S(2)}) collective-permute-start(bf16[64,64,128]{2,1,0:T(8,128)(2,1)} %get-tuple-element.66), channel_id=1, source_target_pairs={{16,0},{32,16},{48,32},{0,48},{80,64},{96,80},{112,96},{64,112},{1... | collective-permute-start | bytes 3145736 | tf_op jit(solution)/shard_map/ppermute | solution.py:133
  8.9 0.9 collective-permute-start.3
  9.8 3.6 %collective-permute-start.8 = (bf16[64,64,128]{2,1,0:T(8,128)(2,1)}, bf16[64,64,128]{2,1,0:T(8,128)(2,1)S(1)}, u32[]{:S(2)}, u32[]{:S(2)}) collective-permute-start(bf16[64,64,128]{2,1,0:T(8,128)(2,1)} %get-tuple-element.76), channel_id=1, source_target_pairs={{0,64},{16,80},{32,96},{48,112},{64,0},{80,16},{96,32},{112,48},{1... | collective-permute-start | bytes 3145736 | tf_op jit(solution)/shard_map/ppermute | solution.py:137
  13.4 0.0 collective-permute-done.ok
  13.4 0.0 collective-permute-start.9
  13.4 0.0 collective-permute-done.1.ov
  13.4 5.5 %attend.1 = bf16[8,576,128]{2,1,0:T(8,128)(2,1)} custom-call(s32[128]{0:T(128)} %old_block.3, s32[64]{0:T(128)} %lengths.1, s32[16]{0:T(128)} %compare_select_fusion.4.base.meta, bf16[64,16,512]{2,1,0:T(8,128)(2,1)} %q, bf16[128,64,128]{2,1,0:T(8,128)(2,1)} %bitcast.13, bf16[128,64,128]{2,1,0:T(8,128)(2,1)} %bitcast.16, ...), custom_call_target="tpu_custom_call" | custom-call | tf_op jit(solution)/shard_map/attend/pallas_call | solution.py:380
  19.0 12.5 %all-to-all-start = ((bf16[8,576,128]{2,1,0:T(8,128)(2,1)}), bf16[8,576,128]{2,1,0:T(8,128)(2,1)S(1)}, u32[]{:S(2)}, u32[]{:S(2)}) async-start(bf16[8,576,128]{2,1,0:T(8,128)(2,1)} %attend.1), calls=%async_computation | async-start | bytes 2359296 | tf_op jit(solution)/shard_map/all_to_all | solution.py:446
  31.4 2.3 %collective-permute-done.2.refs_3_ = bf16[64,64,128]{2,1,0:T(8,128)(2,1)S(1)} collective-permute-done((bf16[64,64,128]{2,1,0:T(8,128)(2,1)}, bf16[64,64,128]{2,1,0:T(8,128)(2,1)S(1)}, u32[]{:S(2)}, u32[]{:S(2)}) %collective-permute-start.2) | collective-permute-done | bytes 1048608 | tf_op jit(solution)/shard_map/ppermute | solution.py:133
  33.7 8.6 %collective-permute-done.3.refs_1_ = bf16[64,64,128]{2,1,0:T(8,128)(2,1)} collective-permute-done((bf16[64,64,128]{2,1,0:T(8,128)(2,1)}, bf16[64,64,128]{2,1,0:T(8,128)(2,1)}, u32[]{:S(2)}, u32[]{:S(2)}) %collective-permute-start.3) | collective-permute-done | bytes 1048608 | tf_op jit(solution)/shard_map/ppermute | solution.py:127
  42.3 0.0 copy-done.2
  42.3 3.7 %shard_map.103 = (bf16[32,64,128]{2,1,0:T(8,128)(2,1)}, bf16[32,64,128]{2,1,0:T(8,128)(2,1)}) custom-call(bf16[32,64,128]{2,1,0:T(8,128)(2,1)} %get-tuple-element.67.refs_0_, bf16[64,64,128]{2,1,0:T(8,128)(2,1)} %collective-permute-done.3.refs_1_, bf16[32,64,128]{2,1,0:T(8,128)(2,1)} %get-tuple-element.69.refs_2_, bf16[64,64,128]{2,1,0:T(8,128)(2,1)} %copy-done.2), custom_call_target="tpu_custom_call" | custom-call | tf_op jit(solution)/shard_map/pallas_call | solution.py:178
  46.0 0.0 collective-permute-start.5
  46.0 12.4 %collective-permute-done.9 = bf16[32,64,128]{2,1,0:T(8,128)(2,1)} collective-permute-done((bf16[32,64,128]{2,1,0:T(8,128)(2,1)}, bf16[32,64,128]{2,1,0:T(8,128)(2,1)}, u32[]{:S(2)}, u32[]{:S(2)}) %collective-permute-start.9) | collective-permute-done | bytes 524320 | tf_op jit(solution)/shard_map/ppermute | solution.py:137
  58.5 1.2 %slice_add_fusion.2 = (bf16[16,64,128]{2,1,0:T(8,128)(2,1)S(1)}, bf16[16,64,128]{2,1,0:T(8,128)(2,1)S(1)}) fusion(bf16[32,64,128]{2,1,0:T(8,128)(2,1)} %collective-permute-done.9, bf16[32,64,128]{2,1,0:T(8,128)(2,1)} %get-tuple-element.78), kind=kLoop, calls=%fused_computation.7 | loop fusion | flops 262144 | bytes 1572864 | tf_op jit(solution)/shard_map/add | solution.py:202
  59.7 2.3 %collective-permute-start.11 = (bf16[16,64,128]{2,1,0:T(8,128)(2,1)S(1)}, bf16[16,64,128]{2,1,0:T(8,128)(2,1)S(1)}, u32[]{:S(2)}, u32[]{:S(2)}) collective-permute-start(bf16[16,64,128]{2,1,0:T(8,128)(2,1)S(1)} %get-tuple-element.86), channel_id=1, source_target_pairs={{16,0},{32,16},{48,32},{0,48},{80,64},{96,80},{112,96},{64,112},{1... | collective-permute-start | bytes 786440 | tf_op jit(solution)/shard_map/ppermute | solution.py:133
  62.0 0.0 collective-permute-start.10
  62.0 3.3 %collective-permute-start.7 = (bf16[32,64,128]{2,1,0:T(8,128)(2,1)}, bf16[32,64,128]{2,1,0:T(8,128)(2,1)S(1)}, u32[]{:S(2)}, u32[]{:S(2)}) collective-permute-start(bf16[32,64,128]{2,1,0:T(8,128)(2,1)} %get-tuple-element.74), channel_id=1, source_target_pairs={{0,64},{16,80},{32,96},{48,112},{64,0},{80,16},{96,32},{112,48},{1... | collective-permute-start | bytes 1572872 | tf_op jit(solution)/shard_map/ppermute | solution.py:137
  65.3 0.0 collective-permute-done.8.refs_1_.refs_3_
  65.3 0.8 collective-permute-done.11.refs_5_
  66.1 3.5 %collective-permute-done.10.refs_4_ = bf16[16,64,128]{2,1,0:T(8,128)(2,1)S(1)} collective-permute-done((bf16[16,64,128]{2,1,0:T(8,128)(2,1)S(1)}, bf16[16,64,128]{2,1,0:T(8,128)(2,1)S(1)}, u32[]{:S(2)}, u32[]{:S(2)}) %collective-permute-start.10) | collective-permute-done | bytes 262176 | tf_op jit(solution)/shard_map/ppermute | solution.py:127
  69.6 0.7 copy-done.7
  70.3 3.9 %shard_map.104 = (bf16[32,64,128]{2,1,0:T(8,128)(2,1)}, bf16[32,64,128]{2,1,0:T(8,128)(2,1)}) custom-call(bf16[32,64,128]{2,1,0:T(8,128)(2,1)} %get-tuple-element.75.refs_0_, bf16[64,64,128]{2,1,0:T(8,128)(2,1)} %copy-done.1, bf16[32,64,128]{2,1,0:T(8,128)(2,1)} %get-tuple-element.77.refs_2_, bf16[64,64,128]{2,1,0:T(8,128)(2,1)} %copy-done.1, ...), custom_call_target="tpu_custom_call" | custom-call | tf_op jit(solution)/shard_map/pallas_call | solution.py:178
  74.2 0.0 collective-permute-start.12
  74.2 3.2 %collective-permute-start.13 = (bf16[32,64,128]{2,1,0:T(8,128)(2,1)}, bf16[32,64,128]{2,1,0:T(8,128)(2,1)}, u32[]{:S(2)}, u32[]{:S(2)}) collective-permute-start(bf16[32,64,128]{2,1,0:T(8,128)(2,1)} %get-tuple-element.81), channel_id=1, source_target_pairs={{16,0},{32,16},{48,32},{0,48},{80,64},{96,80},{112,96},{64,112},{1... | collective-permute-start | bytes 1572872 | tf_op jit(solution)/shard_map/ppermute | solution.py:133
  77.5 0.0 collective-permute-start.4
  77.5 0.0 all-to-all-done.got
  77.5 1.0 copy-done
  78.5 3.1 %join.1 = bf16[8,8,16,512]{3,2,1,0:T(8,128)(2,1)} custom-call(bf16[8,576,128]{2,1,0:T(8,128)(2,1)} %copy-done), custom_call_target="tpu_custom_call" | custom-call | tf_op jit(solution)/shard_map/join/pallas_call | solution.py:436
  81.6 7.3 %all-to-all-start.1 = ((bf16[8,8,16,512]{3,2,1,0:T(8,128)(2,1)}), bf16[8,8,16,512]{3,2,1,0:T(8,128)(2,1)S(1)}, u32[]{:S(2)}, u32[]{:S(2)}) async-start(bf16[8,8,16,512]{3,2,1,0:T(8,128)(2,1)} %join.1), calls=%async_computation.1 | async-start | bytes 2097152 | tf_op jit(solution)/shard_map/all_to_all | solution.py:446
  88.8 0.0 copy-start.4
  88.9 0.0 collective-permute-done.5
  88.9 1.6 %fusion = bf16[32,64,128]{2,1,0:T(8,128)(2,1)S(1)} fusion(bf16[32,64,128]{2,1,0:T(8,128)(2,1)} %collective-permute-done.5, bf16[32,64,128]{2,1,0:T(8,128)(2,1)} %get-tuple-element.71, bf16[64,64,128]{2,1,0:T(8,128)(2,1)} %collective-permute-done.3.refs_1_), kind=kLoop, calls=%fused_computation.1 | loop fusion | flops 524288 | bytes 2097152 | tf_op jit(solution)/shard_map/add | solution.py:193
  90.4 3.6 %collective-permute-start.6 = (bf16[32,64,128]{2,1,0:T(8,128)(2,1)S(1)}, bf16[32,64,128]{2,1,0:T(8,128)(2,1)S(1)}, u32[]{:S(2)}, u32[]{:S(2)}) collective-permute-start(bf16[32,64,128]{2,1,0:T(8,128)(2,1)S(1)} %fusion), channel_id=1, source_target_pairs={{0,64},{16,80},{32,96},{48,112},{64,0},{80,16},{96,32},{112,48},{1... | collective-permute-start | bytes 1572872 | tf_op jit(solution)/shard_map/ppermute | solution.py:137
  94.0 0.0 collective-permute-done.7
  94.0 0.0 collective-permute-done.12
  94.0 0.0 collective-permute-done.13
  94.0 2.1 %add_bitcast_fusion = bf16[32,1,64,128]{3,2,1,0:T(8,128)(2,1)} fusion(bf16[32,64,128]{2,1,0:T(8,128)(2,1)} %collective-permute-done.13, bf16[32,64,128]{2,1,0:T(8,128)(2,1)} %collective-permute-done.12, bf16[32,64,128]{2,1,0:T(8,128)(2,1)S(1)} %copy-done.5, bf16[32,64,128]{2,1,0:T(8,128)(2,1)S(1)} %collective-permute-done.7), kind=kLoop, calls=%fused_computation.6 | loop fusion | flops 786432 | bytes 2621440
  96.1 8.9 %collective-permute-done.4 = bf16[32,64,128]{2,1,0:T(8,128)(2,1)} collective-permute-done((bf16[32,64,128]{2,1,0:T(8,128)(2,1)}, bf16[32,64,128]{2,1,0:T(8,128)(2,1)}, u32[]{:S(2)}, u32[]{:S(2)}) %collective-permute-start.4) | collective-permute-done | bytes 524320 | tf_op jit(solution)/shard_map/ppermute | solution.py:127
  105.0 3.9 %collective-permute-done.6 = bf16[32,64,128]{2,1,0:T(8,128)(2,1)S(1)} collective-permute-done((bf16[32,64,128]{2,1,0:T(8,128)(2,1)S(1)}, bf16[32,64,128]{2,1,0:T(8,128)(2,1)S(1)}, u32[]{:S(2)}, u32[]{:S(2)}) %collective-permute-start.6) | collective-permute-done | bytes 524320 | tf_op jit(solution)/shard_map/ppermute | solution.py:137
  109.0 0.0 copy-done.4
  109.0 1.9 %fusion.3 = bf16[32,1,64,128]{3,2,1,0:T(8,128)(2,1)} fusion(bf16[32,64,128]{2,1,0:T(8,128)(2,1)S(1)} %collective-permute-done.6, bf16[32,64,128]{2,1,0:T(8,128)(2,1)} %collective-permute-done.4, bf16[32,64,128]{2,1,0:T(8,128)(2,1)S(1)} %copy-done.4, bf16[64,64,128]{2,1,0:T(8,128)(2,1)S(1)} %copy-done.3), kind=kLoop, calls=%fused_computation.5 | loop fusion | flops 786432 | bytes 2621440
  110.9 0.0 all-to-all-done.1
  110.9 1.0 copy.14
  (11 shorter events, 0.0 us)
Async XLA Ops:
  0.6 12.8 %collective-permute-start = (bf16[128,64,128]{2,1,0:T(8,128)(2,1)}, bf16[128,64,128]{2,1,0:T(8,128)(2,1)}, u32[]{:S(2)}, u32[]{:S(2)}) collective-permute-start(bf16[128,64,128]{2,1,0:T(8,128)(2,1)} %bitcast.11), channel_id=1, source_target_pairs={{0,1},{1,0},{2,3},{3,2},{4,5},{5,4},{6,7},{7,6},{8,9},{9,8},{10,11... | collective-permute-start | bytes 6291464 | tf_op jit(solution)/shard_map/ppermute | solution.py:460
  0.7 12.7 %collective-permute-start.1 = (bf16[128,64,128]{2,1,0:T(8,128)(2,1)}, bf16[128,64,128]{2,1,0:T(8,128)(2,1)}, u32[]{:S(2)}, u32[]{:S(2)}) collective-permute-start(bf16[128,64,128]{2,1,0:T(8,128)(2,1)} %bitcast.14), channel_id=1, source_target_pairs={{0,1},{1,0},{2,3},{3,2},{4,5},{5,4},{6,7},{7,6},{8,9},{9,8},{10,11... | collective-permute-start | bytes 6291464 | tf_op jit(solution)/shard_map/ppermute | solution.py:461
  6.0 27.7 %collective-permute-start.2 = (bf16[64,64,128]{2,1,0:T(8,128)(2,1)}, bf16[64,64,128]{2,1,0:T(8,128)(2,1)S(1)}, u32[]{:S(2)}, u32[]{:S(2)}) collective-permute-start(bf16[64,64,128]{2,1,0:T(8,128)(2,1)} %get-tuple-element.66), channel_id=1, source_target_pairs={{16,0},{32,16},{48,32},{0,48},{80,64},{96,80},{112,96},{64,112},{1... | collective-permute-start | bytes 3145736 | tf_op jit(solution)/shard_map/ppermute | solution.py:133
  8.9 33.4 %collective-permute-start.3 = (bf16[64,64,128]{2,1,0:T(8,128)(2,1)}, bf16[64,64,128]{2,1,0:T(8,128)(2,1)}, u32[]{:S(2)}, u32[]{:S(2)}) collective-permute-start(bf16[64,64,128]{2,1,0:T(8,128)(2,1)} %get-tuple-element.68), channel_id=1, source_target_pairs={{0,16},{16,32},{32,48},{48,0},{64,80},{80,96},{96,112},{112,64},{1... | collective-permute-start | bytes 3145736 | tf_op jit(solution)/shard_map/ppermute | solution.py:127
  9.8 55.6 %collective-permute-start.8 = (bf16[64,64,128]{2,1,0:T(8,128)(2,1)}, bf16[64,64,128]{2,1,0:T(8,128)(2,1)S(1)}, u32[]{:S(2)}, u32[]{:S(2)}) collective-permute-start(bf16[64,64,128]{2,1,0:T(8,128)(2,1)} %get-tuple-element.76), channel_id=1, source_target_pairs={{0,64},{16,80},{32,96},{48,112},{64,0},{80,16},{96,32},{112,48},{1... | collective-permute-start | bytes 3145736 | tf_op jit(solution)/shard_map/ppermute | solution.py:137
  13.4 45.0 %collective-permute-start.9 = (bf16[32,64,128]{2,1,0:T(8,128)(2,1)}, bf16[32,64,128]{2,1,0:T(8,128)(2,1)}, u32[]{:S(2)}, u32[]{:S(2)}) collective-permute-start(bf16[32,64,128]{2,1,0:T(8,128)(2,1)} %get-tuple-element.79), channel_id=1, source_target_pairs={{0,64},{16,80},{32,96},{48,112},{64,0},{80,16},{96,32},{112,48},{1... | collective-permute-start | bytes 1572872 | tf_op jit(solution)/shard_map/ppermute | solution.py:137
  19.0 58.5 %all-to-all-start = ((bf16[8,576,128]{2,1,0:T(8,128)(2,1)}), bf16[8,576,128]{2,1,0:T(8,128)(2,1)S(1)}, u32[]{:S(2)}, u32[]{:S(2)}) async-start(bf16[8,576,128]{2,1,0:T(8,128)(2,1)} %attend.1), calls=%async_computation | async-start | bytes 2359296 | tf_op jit(solution)/shard_map/all_to_all | solution.py:446
  33.7 8.6 %copy-start.2 = (bf16[64,64,128]{2,1,0:T(8,128)(2,1)}, bf16[64,64,128]{2,1,0:T(8,128)(2,1)S(1)}, u32[]{:S(2)}) copy-start(bf16[64,64,128]{2,1,0:T(8,128)(2,1)S(1)} %collective-permute-done.2.refs_3_) | copy-start | bytes 3145732
  46.0 42.8 %collective-permute-start.5 = (bf16[32,64,128]{2,1,0:T(8,128)(2,1)}, bf16[32,64,128]{2,1,0:T(8,128)(2,1)}, u32[]{:S(2)}, u32[]{:S(2)}) collective-permute-start(bf16[32,64,128]{2,1,0:T(8,128)(2,1)} %get-tuple-element.72), channel_id=1, source_target_pairs={{16,0},{32,16},{48,32},{0,48},{80,64},{96,80},{112,96},{64,112},{1... | collective-permute-start | bytes 1572872 | tf_op jit(solution)/shard_map/ppermute | solution.py:133
  59.7 6.4 %collective-permute-start.11 = (bf16[16,64,128]{2,1,0:T(8,128)(2,1)S(1)}, bf16[16,64,128]{2,1,0:T(8,128)(2,1)S(1)}, u32[]{:S(2)}, u32[]{:S(2)}) collective-permute-start(bf16[16,64,128]{2,1,0:T(8,128)(2,1)S(1)} %get-tuple-element.86), channel_id=1, source_target_pairs={{16,0},{32,16},{48,32},{0,48},{80,64},{96,80},{112,96},{64,112},{1... | collective-permute-start | bytes 786440 | tf_op jit(solution)/shard_map/ppermute | solution.py:133
  62.0 7.6 %collective-permute-start.10 = (bf16[16,64,128]{2,1,0:T(8,128)(2,1)S(1)}, bf16[16,64,128]{2,1,0:T(8,128)(2,1)S(1)}, u32[]{:S(2)}, u32[]{:S(2)}) collective-permute-start(bf16[16,64,128]{2,1,0:T(8,128)(2,1)S(1)} %get-tuple-element.87), channel_id=1, source_target_pairs={{0,16},{16,32},{32,48},{48,0},{64,80},{80,96},{96,112},{112,64},{1... | collective-permute-start | bytes 786440 | tf_op jit(solution)/shard_map/ppermute | solution.py:127
  62.0 32.0 %collective-permute-start.7 = (bf16[32,64,128]{2,1,0:T(8,128)(2,1)}, bf16[32,64,128]{2,1,0:T(8,128)(2,1)S(1)}, u32[]{:S(2)}, u32[]{:S(2)}) collective-permute-start(bf16[32,64,128]{2,1,0:T(8,128)(2,1)} %get-tuple-element.74), channel_id=1, source_target_pairs={{0,64},{16,80},{32,96},{48,112},{64,0},{80,16},{96,32},{112,48},{1... | collective-permute-start | bytes 1572872 | tf_op jit(solution)/shard_map/ppermute | solution.py:137
  65.3 4.3 %copy-start.1 = (bf16[64,64,128]{2,1,0:T(8,128)(2,1)}, bf16[64,64,128]{2,1,0:T(8,128)(2,1)S(1)}, u32[]{:S(2)}) copy-start(bf16[64,64,128]{2,1,0:T(8,128)(2,1)S(1)} %collective-permute-done.8.refs_1_.refs_3_) | copy-start | bytes 3145732
  66.1 3.5 %copy-start.6 = (bf16[16,64,128]{2,1,0:T(8,128)(2,1)}, bf16[16,64,128]{2,1,0:T(8,128)(2,1)S(1)}, u32[]{:S(2)}) copy-start(bf16[16,64,128]{2,1,0:T(8,128)(2,1)S(1)} %collective-permute-done.11.refs_5_) | copy-start | bytes 786436
  69.6 0.7 copy-start.7
  74.2 19.8 %collective-permute-start.12 = (bf16[32,64,128]{2,1,0:T(8,128)(2,1)}, bf16[32,64,128]{2,1,0:T(8,128)(2,1)}, u32[]{:S(2)}, u32[]{:S(2)}) collective-permute-start(bf16[32,64,128]{2,1,0:T(8,128)(2,1)} %get-tuple-element.80), channel_id=1, source_target_pairs={{0,16},{16,32},{32,48},{48,0},{64,80},{80,96},{96,112},{112,64},{1... | collective-permute-start | bytes 1572872 | tf_op jit(solution)/shard_map/ppermute | solution.py:127
  74.2 19.8 %collective-permute-start.13 = (bf16[32,64,128]{2,1,0:T(8,128)(2,1)}, bf16[32,64,128]{2,1,0:T(8,128)(2,1)}, u32[]{:S(2)}, u32[]{:S(2)}) collective-permute-start(bf16[32,64,128]{2,1,0:T(8,128)(2,1)} %get-tuple-element.81), channel_id=1, source_target_pairs={{16,0},{32,16},{48,32},{0,48},{80,64},{96,80},{112,96},{64,112},{1... | collective-permute-start | bytes 1572872 | tf_op jit(solution)/shard_map/ppermute | solution.py:133
  77.5 27.6 %collective-permute-start.4 = (bf16[32,64,128]{2,1,0:T(8,128)(2,1)}, bf16[32,64,128]{2,1,0:T(8,128)(2,1)}, u32[]{:S(2)}, u32[]{:S(2)}) collective-permute-start(bf16[32,64,128]{2,1,0:T(8,128)(2,1)} %get-tuple-element.70), channel_id=1, source_target_pairs={{0,16},{16,32},{32,48},{48,0},{64,80},{80,96},{96,112},{112,64},{1... | collective-permute-start | bytes 1572872 | tf_op jit(solution)/shard_map/ppermute | solution.py:127
  77.5 1.0 copy-start
  81.6 12.5 %copy-start.5 = (bf16[32,64,128]{2,1,0:T(8,128)(2,1)S(1)}, bf16[32,64,128]{2,1,0:T(8,128)(2,1)}, u32[]{:S(2)}) copy-start(bf16[32,64,128]{2,1,0:T(8,128)(2,1)} %get-tuple-element.73) | copy-start | bytes 1572868
  81.6 29.3 %all-to-all-start.1 = ((bf16[8,8,16,512]{3,2,1,0:T(8,128)(2,1)}), bf16[8,8,16,512]{3,2,1,0:T(8,128)(2,1)S(1)}, u32[]{:S(2)}, u32[]{:S(2)}) async-start(bf16[8,8,16,512]{3,2,1,0:T(8,128)(2,1)} %join.1), calls=%async_computation.1 | async-start | bytes 2097152 | tf_op jit(solution)/shard_map/all_to_all | solution.py:446
  88.8 20.1 %copy-start.3 = (bf16[64,64,128]{2,1,0:T(8,128)(2,1)S(1)}, bf16[64,64,128]{2,1,0:T(8,128)(2,1)}, u32[]{:S(2)}) copy-start(bf16[64,64,128]{2,1,0:T(8,128)(2,1)} %copy-done.2) | copy-start | bytes 3145732
  88.8 20.1 %copy-start.4 = (bf16[32,64,128]{2,1,0:T(8,128)(2,1)S(1)}, bf16[32,64,128]{2,1,0:T(8,128)(2,1)}, u32[]{:S(2)}) copy-start(bf16[32,64,128]{2,1,0:T(8,128)(2,1)} %get-tuple-element.65) | copy-start | bytes 1572868
  90.4 18.5 %collective-permute-start.6 = (bf16[32,64,128]{2,1,0:T(8,128)(2,1)S(1)}, bf16[32,64,128]{2,1,0:T(8,128)(2,1)S(1)}, u32[]{:S(2)}, u32[]{:S(2)}) collective-permute-start(bf16[32,64,128]{2,1,0:T(8,128)(2,1)S(1)} %fusion), channel_id=1, source_target_pairs={{0,64},{16,80},{32,96},{48,112},{64,0},{80,16},{96,32},{112,48},{1... | collective-permute-start | bytes 1572872 | tf_op jit(solution)/shard_map/ppermute | solution.py:137
